TPU v7x, 32 devices: a whole 2x2x4 slice. The times are simulated.
32 devices in a mesh: grp: 4 (over z), dev: 8 (over y, x, core).
Axes of the slice: x: 2, y: 2, z: 4, core: 2. Of those that a mesh axis runs over, the one named last changes fastest.
Arguments:
- a_blocks: bfloat16 [1024, 7, 192, 192], P(('grp', 'dev')), may hold values from -0.4375 to 0.4375
- prolong_t: bfloat16 [1024, 32, 192], P(('grp', 'dev')), may hold values from -1.796875 to 1.796875
- elem_slot: int32 [1024], P(('grp', 'dev')), may hold values from 0 to 5, as said below
- touch_agg: int32 [32, 6], replicated, may hold values from 0 to 135, as said below
- nbr: int32 [1024, 6], P(('grp', 'dev')), may hold values from -1 to 1023, as said below
- nbr_agg: int32 [1024, 6], P(('grp', 'dev')), may hold values from -1 to 135, as said below
- coarse_row: int32 [136], replicated, may hold values from 0 to 191, as said below
Outputs:
- coarse: float32 [192, 7, 1024], P('dev')
Inputs may be any that keep to these rules, and one draw needn't show every extreme that they name: Element e lies on device e // 32 (devices numbered grp-major). elem_slot[e] is the position of e's aggregate in touch_agg[e // 32]. `touch_agg`: each row lists 6 distinct aggregates, exactly those of the device's elements; all devices that touch one aggregate share their grp index. `nbr`: global element index across each face, or -1 on the domain's boundary; adjacency is symmetric; a neighbour lies on the same device, or on the device whose grp index differs by one (same dev index), or whose dev index differs by one (same grp index); exactly 8 elements of a device have a neighbour on each existing device next along grp, and exactly 8 on each existing device next along dev. `nbr_agg`: the aggregate of the element nbr[e, f], -1 exactly where nbr[e, f] is -1. Distinct values; aggregate a's row belongs to dev index coarse_row[a] // 24. Of the aggregates touched by one device at most 1 belong to one dev index, and of those touched by the devices of one grp index at most 6; one dev index reaches both bounds and holds 24 rows.
All inputs are finite; a program needn't handle non-finite values.
Results may differ from a plain program's by a relative error of at most 0.005.
Values may be sent and summed in bfloat16 or wider, within the bound.
A program may use at most 128 MiB of HBM per device.

v0:
```python
import functools

import jax
import jax.numpy as jnp
from jax import lax
from jax.experimental import pallas as pl
from jax.experimental.pallas import tpu as pltpu
from jax.sharding import PartitionSpec as P

EX = 4
EY = 4
MESH = pl.DeviceIdType.MESH
F32 = jnp.float32
BF16 = jnp.bfloat16


def iota(shape, dim):
    return lax.broadcasted_iota(jnp.int32, shape, dim)


def tables(
    n_grp, n_dev, halo, group_rows, rows_own,
    nbr, nbr_agg, slot, touch_agg, coarse_row,
    tab, ms, ma,
):
    grp = lax.axis_index("grp")
    dev = lax.axis_index("dev")
    device = grp * n_dev + dev
    faces, e_dev = nbr.shape
    devices, touch = touch_agg.shape
    wide = ms.shape[1]
    width_c = wide // (faces + 1)

    def where_sum(mask, value, axis):
        return jnp.sum(jnp.where(mask, value, 0), axis=axis, keepdims=True)

    def put(row, value):
        tab[row:row + value.shape[0], 0:value.shape[1]] = value

    near = [
        jnp.where(grp > 0, device - n_dev, -2),
        jnp.where(grp < n_grp - 1, device + n_dev, -2),
        jnp.where(dev > 0, device - 1, -2),
        jnp.where(dev < n_dev - 1, device + 1, -2),
    ]
    ids = nbr[...]
    source = jnp.where(ids >= 0, jnp.maximum(ids, 0) // e_dev, -1)
    local = ids - source * e_dev
    hits = [jnp.max(jnp.where(source == n, 1.0, 0.0), axis=0, keepdims=True) for n in near]
    below = jnp.where(iota((e_dev, e_dev), 0) < iota((e_dev, e_dev), 1), 1.0, 0.0).astype(BF16)
    rank = jnp.dot(
        jnp.concatenate(hits + hits, axis=0).astype(BF16), below, preferred_element_type=F32
    ).astype(jnp.int32)
    lanes = iota((halo, e_dev), 1)
    for d in range(4):
        found = (rank[d:d + 1] == iota((halo, e_dev), 0)) & (hits[d] > 0)
        tab[8:8 + halo, d:d + 1] = where_sum(found, lanes, 1)
    index = iota((e_dev, e_dev), 0)
    where_from = [jnp.where(source[f:f + 1] == device, local[f:f + 1], 0) for f in range(faces)]
    for d in range(4):
        seen = jnp.zeros((e_dev, e_dev), jnp.int32)
        for f in range(faces):
            seen = jnp.where(ids[f:f + 1] == near[d] * e_dev + index, 1, seen)
        seen = jnp.max(seen, axis=1, keepdims=True)
        for f in range(faces):
            ahead = where_sum(index < local[f:f + 1], seen, 0)
            where_from[f] = jnp.where(
                source[f:f + 1] == near[d], e_dev + d * halo + ahead, where_from[f]
            )
    for f in range(faces):
        put(f, where_from[f])

    row = iota((devices, 1), 0)
    entries = touch_agg[...]
    columns = [entries[:, t:t + 1] for t in range(touch)]
    slots = slot[...]
    put(19, slots)
    own_agg = jnp.zeros((1, e_dev), jnp.int32)
    for t in range(touch):
        own_agg = jnp.where(slots == t, where_sum(row == device, columns[t], 0), own_agg)
    valid = ids >= 0
    same = valid & (nbr_agg[...] == own_agg)
    apart = jnp.where(valid & jnp.logical_not(same), 1.0, 0.0).astype(BF16)
    same = jnp.where(same, 1.0, 0.0).astype(BF16)
    unit = jnp.where(iota((e_dev, e_dev), 0) == iota((e_dev, e_dev), 1), 1.0, 0.0).astype(BF16)
    group = jnp.where(iota((faces, wide), 1) // width_c == iota((faces, wide), 0) + 1, 1.0, 0.0).astype(BF16)

    def expand(flags):
        turned = lax.dot_general(unit, flags, (((1,), (1,)), ((), ())), preferred_element_type=F32)
        return jnp.dot(turned.astype(BF16), group, preferred_element_type=F32)

    ms[...] = expand(same) + jnp.where(iota((e_dev, wide), 1) < width_c, 1.0, 0.0)
    ma[...] = expand(apart)

    n_agg = coarse_row.shape[1]
    numbers = coarse_row[...]
    across = iota((devices, n_agg), 1)
    targets = [where_sum(columns[t] == across, numbers, 1) for t in range(touch)]
    owners = [target // rows_own for target in targets]
    lane = iota((devices, rows_own), 1)
    present = jnp.zeros((devices, rows_own), F32)
    for t in range(touch):
        here = jnp.where(owners[t] == dev, targets[t] - owners[t] * rows_own, -1)
        present = jnp.where(here == lane, 1.0, present)
    mates = jnp.where(
        iota((devices, devices), 0) // n_dev == iota((devices, devices), 1) // n_dev, 1.0, 0.0
    ).astype(BF16)
    shared = jnp.dot(mates, present.astype(BF16), preferred_element_type=F32) > 0
    shared = jnp.where(shared, 1.0, 0.0)
    lower = jnp.where(
        iota((rows_own, rows_own), 0) < iota((rows_own, rows_own), 1), 1.0, 0.0
    ).astype(BF16)
    order = jnp.dot(shared.astype(BF16), lower, preferred_element_type=F32)
    heads = where_sum(row % n_dev == 0, shared * (order + 1.0 + (row // n_dev * group_rows).astype(F32)), 0)
    put(16, heads.astype(jnp.int32) - 1)
    spots = jnp.sum(present * (order + 1.0), axis=1, keepdims=True).astype(jnp.int32) - 1
    peer = iota((devices, n_dev), 1) + grp * n_dev
    put(18, where_sum(peer == iota((devices, n_dev), 0), spots, 0))
    inverse = jnp.full((1, n_dev), touch, jnp.int32)
    for t in range(touch):
        own = where_sum(row == device, owners[t], 0)
        inverse = jnp.where(own == iota((1, n_dev), 1), t, inverse)
    put(17, inverse)


def finish(group_rows, tab, gathered, out_ref, flat):
    rows_own, n_k, row_width = out_ref.shape
    lane = 128
    sub = row_width // lane

    @pl.loop(0, rows_own, unroll=4)
    def _(r):
        at = tab[16, r]
        safe = jnp.maximum(at, 0)
        row = gathered[safe // group_rows, safe % group_rows].astype(F32)
        flat[r] = jnp.where(at >= 0, row, 0.0)
        for j in range(sub):
            out_ref[r, :, j * lane:(j + 1) * lane] = flat[r, pl.ds(j, n_k, stride=sub), :]


def kernel(
    n_grp, n_dev, halo, group_rows,
    tab, a_ref, p_ref, ms_ref, ma_ref,
    gathered,
    a_buf, pool, pack, left, prod_s, prod_a, part_t, parts, inbox,
    a_sem, h_send, h_recv, x_send, x_recv, g_send, g_recv,
):
    grp = lax.axis_index("grp")
    dev = lax.axis_index("dev")
    e_dev, width_c, width_b = p_ref.shape
    n_k = a_ref.shape[1]
    touch = part_t.shape[0] - 1
    wide = n_k * width_c
    lane = 128
    rep = lane // width_c
    sub = width_c // rep

    def a_copy(e):
        return pltpu.make_async_copy(a_ref.at[e], a_buf.at[e], a_sem.at[e])

    @pl.loop(0, e_dev)
    def _(e):
        a_copy(e).start()

    barrier = pltpu.get_barrier_semaphore()
    for off in range(1, n_dev):
        pl.semaphore_signal(
            barrier, inc=1, device_id=(grp, lax.rem(dev + off, n_dev)), device_id_type=MESH
        )
    for off in range(1, n_grp):
        pl.semaphore_signal(
            barrier, inc=1, device_id=(lax.rem(grp + off, n_grp), dev), device_id_type=MESH
        )

    for j in range(4 * halo):
        pack[j] = p_ref[tab[8 + j % halo, j // halo]]
    pool[0:e_dev] = p_ref[...]
    pl.semaphore_wait(barrier, n_dev + n_grp - 2)

    dirs = (
        (grp > 0, (grp - 1, dev)),
        (grp < n_grp - 1, (grp + 1, dev)),
        (dev > 0, (grp, dev - 1)),
        (dev < n_dev - 1, (grp, dev + 1)),
    )

    def halo_copy(d, target):
        back = d ^ 1
        return pltpu.make_async_remote_copy(
            src_ref=pack.at[pl.ds(d * halo, halo)],
            dst_ref=pool.at[pl.ds(e_dev + back * halo, halo)],
            send_sem=h_send.at[d],
            recv_sem=h_recv.at[back],
            device_id=target,
            device_id_type=MESH,
        )

    for d, (there, target) in enumerate(dirs):
        @pl.when(there)
        def _(d=d, target=target):
            halo_copy(d, target).start()

    @pl.loop(0, e_dev, unroll=2)
    def _(e):
        a_copy(e).wait()
        own = p_ref[e]
        for k in range(n_k):
            left[e, k * width_c:(k + 1) * width_c, :] = jnp.dot(
                own, a_buf[e, k], preferred_element_type=F32
            ).astype(BF16)

    for d, (there, target) in enumerate(dirs):
        @pl.when(there)
        def _(d=d, target=target):
            halo_copy(d, target).wait_send()
            pltpu.make_async_remote_copy(
                src_ref=pack.at[pl.ds(d * halo, halo)],
                dst_ref=pool.at[pl.ds(e_dev + d * halo, halo)],
                send_sem=h_send.at[d],
                recv_sem=h_recv.at[d],
                device_id=target,
                device_id_type=MESH,
            ).wait_recv()

    group_of_lane = iota((width_c, wide), 1) // width_c

    @pl.loop(0, e_dev, unroll=4)
    def _(e):
        right = jnp.concatenate(
            [pool[e]] + [pool[tab[f, e]] for f in range(n_k - 1)], axis=0
        )
        full = lax.dot_general(
            left[e], right, (((1,), (1,)), ((), ())), preferred_element_type=F32
        )
        picked = full[0:width_c]
        for k in range(1, n_k):
            picked = jnp.where(group_of_lane == k, full[k * width_c:(k + 1) * width_c], picked)
        prod_s[e] = jnp.where(ms_ref[pl.ds(e, 1), :] > 0, picked, 0.0)
        prod_a[e] = jnp.where(ma_ref[pl.ds(e, 1), :] > 0, picked, 0.0)

    spread_s = (iota((wide, lane), 0) % width_c == iota((wide, lane), 1) % width_c).astype(F32).astype(BF16)
    rest = (n_k - 1) * lane
    spread_a = (
        iota((wide, rest), 0)
        == (iota((wide, rest), 1) // lane + 1) * width_c + iota((wide, rest), 1) % width_c
    ).astype(F32).astype(BF16)
    keep = iota((width_c, n_k * lane), 0) % rep == (iota((width_c, n_k * lane), 1) % lane) // width_c
    squeeze = (iota((sub, width_c), 1) // rep == iota((sub, width_c), 0)).astype(F32).astype(BF16)

    part_t[touch] = jnp.zeros(part_t.shape[1:], BF16)

    def spread(value, table):
        high = value.astype(BF16)
        low = (value - high.astype(F32)).astype(BF16)
        return jnp.dot(high, table, preferred_element_type=F32) + jnp.dot(
            low, table, preferred_element_type=F32
        )

    for t in range(touch):
        zero = jnp.zeros((width_c, wide), F32)

        def add(e, sums, t=t):
            sum_s, sum_a = sums
            member = jnp.where(tab[19, e] == t, 1.0, 0.0).astype(F32)
            return sum_s + prod_s[e] * member, sum_a + prod_a[e] * member

        sum_s, sum_a = lax.fori_loop(0, e_dev, add, (zero, zero), unroll=8)
        both = jnp.concatenate([spread(sum_s, spread_s), spread(sum_a, spread_a)], axis=1)
        both = jnp.where(keep, both, 0.0).astype(BF16)
        rows = jnp.dot(squeeze, both, preferred_element_type=F32)
        rows = jnp.concatenate([rows[:, s * lane:(s + 1) * lane] for s in range(n_k)], axis=0)
        part_t[t] = rows.astype(BF16)

    for o in range(n_dev):
        parts[o] = part_t[tab[17, o]]
    inbox[dev] = parts[dev]

    def part_copy(off):
        target = lax.rem(dev + off, n_dev)
        return pltpu.make_async_remote_copy(
            src_ref=parts.at[target],
            dst_ref=inbox.at[dev],
            send_sem=x_send.at[off],
            recv_sem=x_recv.at[off],
            device_id=(grp, target),
            device_id_type=MESH,
        )

    def part_arrival(off):
        sender = lax.rem(dev + n_dev - off, n_dev)
        return pltpu.make_async_remote_copy(
            src_ref=parts.at[sender],
            dst_ref=inbox.at[sender],
            send_sem=x_send.at[off],
            recv_sem=x_recv.at[off],
            device_id=(grp, sender),
            device_id_type=MESH,
        )

    for off in range(1, n_dev):
        part_copy(off).start()
    for off in range(1, n_dev):
        part_arrival(off).wait_recv()

    for j in range(group_rows):
        total = jnp.zeros(parts.shape[1:], F32)
        for d in range(n_dev):
            member = jnp.where(tab[18, d] == j, 1.0, 0.0).astype(F32)
            total = total + inbox[d].astype(F32) * member
        gathered[grp, j] = total.astype(BF16)

    def row_copy(off):
        target = lax.rem(grp + off, n_grp)
        return pltpu.make_async_remote_copy(
            src_ref=gathered.at[grp],
            dst_ref=gathered.at[grp],
            send_sem=g_send.at[off],
            recv_sem=g_recv.at[off],
            device_id=(target, dev),
            device_id_type=MESH,
        )

    def row_arrival(off):
        sender = lax.rem(grp + n_grp - off, n_grp)
        return pltpu.make_async_remote_copy(
            src_ref=gathered.at[sender],
            dst_ref=gathered.at[sender],
            send_sem=g_send.at[off],
            recv_sem=g_recv.at[off],
            device_id=(sender, dev),
            device_id_type=MESH,
        )

    for off in range(1, n_grp):
        row_copy(off).start()
    for off in range(1, n_grp):
        row_arrival(off).wait_recv()

    for off in range(1, n_dev):
        part_copy(off).wait_send()
    for off in range(1, n_grp):
        row_copy(off).wait_send()


def on_device(n_grp, n_dev, a_blocks, prolong_t, elem_slot, touch_agg, nbr, nbr_agg, coarse_row):
    e_dev, width_c, width_b = prolong_t.shape
    n_k = a_blocks.shape[1]
    touch = touch_agg.shape[1]
    halo = e_dev // EX
    half_y = EY // 2
    span_y = half_y + 1
    group_rows = (n_dev * half_y + 1 + half_y) // span_y
    rows_own = n_grp * group_rows
    assert touch <= n_dev
    lane = 128
    flat_rows = n_k * width_c * width_c // lane
    smem = pl.BlockSpec(memory_space=pltpu.SMEM)
    vmem = pl.BlockSpec(memory_space=pltpu.VMEM)
    wide = n_k * width_c
    tab, ms, ma = pl.pallas_call(
        functools.partial(tables, n_grp, n_dev, halo, group_rows, rows_own),
        out_shape=(
            jax.ShapeDtypeStruct((24, lane), jnp.int32),
            jax.ShapeDtypeStruct((e_dev, wide), F32),
            jax.ShapeDtypeStruct((e_dev, wide), F32),
        ),
        in_specs=[vmem] * 5,
        out_specs=(vmem, vmem, vmem),
        name="index_tables",
    )(nbr.T, nbr_agg.T, elem_slot.reshape(1, e_dev), touch_agg, coarse_row.reshape(1, -1))
    gathered = pl.pallas_call(
        functools.partial(kernel, n_grp, n_dev, halo, group_rows),
        out_shape=jax.ShapeDtypeStruct((n_grp, group_rows, flat_rows, lane), BF16),
        in_specs=[smem, pl.BlockSpec(memory_space=pl.ANY)] + [vmem] * 3,
        out_specs=vmem,
        scratch_shapes=[
            pltpu.VMEM(a_blocks.shape, BF16),
            pltpu.VMEM((e_dev + 4 * halo, width_c, width_b), BF16),
            pltpu.VMEM((4 * halo, width_c, width_b), BF16),
            pltpu.VMEM((e_dev, wide, width_b), BF16),
            pltpu.VMEM((e_dev, width_c, wide), F32),
            pltpu.VMEM((e_dev, width_c, wide), F32),
            pltpu.VMEM((touch + 1, flat_rows, lane), BF16),
            pltpu.VMEM((n_dev, flat_rows, lane), BF16),
            pltpu.VMEM((n_dev, flat_rows, lane), BF16),
            pltpu.SemaphoreType.DMA((e_dev,)),
            pltpu.SemaphoreType.DMA((4,)),
            pltpu.SemaphoreType.DMA((4,)),
            pltpu.SemaphoreType.DMA((n_dev,)),
            pltpu.SemaphoreType.DMA((n_dev,)),
            pltpu.SemaphoreType.DMA((n_grp,)),
            pltpu.SemaphoreType.DMA((n_grp,)),
        ],
        compiler_params=pltpu.CompilerParams(
            collective_id=0, has_side_effects=True, vmem_limit_bytes=60 * 1024 * 1024
        ),
        name="galerkin",
    )(tab, a_blocks, prolong_t, ms, ma)
    return pl.pallas_call(
        functools.partial(finish, group_rows),
        out_shape=jax.ShapeDtypeStruct((rows_own, n_k, width_c * width_c), F32),
        in_specs=[smem, vmem],
        out_specs=vmem,
        scratch_shapes=[pltpu.VMEM((rows_own, flat_rows, lane), F32)],
        name="index_finish",
    )(tab, gathered)


def solution(mesh):
    in_specs = (
        P(("grp", "dev"), None, None, None),
        P(("grp", "dev"), None, None),
        P(("grp", "dev")),
        P(),
        P(("grp", "dev"), None),
        P(("grp", "dev"), None),
        P(),
    )
    out_specs = P("dev", None, None)
    return jax.shard_map(
        functools.partial(on_device, mesh.shape["grp"], mesh.shape["dev"]),
        mesh=mesh, in_specs=in_specs, out_specs=out_specs, check_vma=False,
    )
```

profile of v0, /device:TPU:0, one launch (start us, length us, event | category | flops | bytes accessed | tf_op | source)
XLA Modules:
  0.0 41.6 jit_solution(10188723357708375308)
XLA Ops:
  0.0 1.4 %copy.8.touch_agg = s32[32,6]{1,0:T(8,128)} copy(s32[32,6]{0,1:T(8,128)} %param.10) | data formatting | bytes 1536 | tf_op args[3]
  1.4 2.0 %index_tables.1 = (s32[24,128]{1,0:T(8,128)}, f32[32,224]{1,0:T(8,128)}, f32[32,224]{1,0:T(8,128)}) custom-call(s32[6,32]{1,0:T(8,128)} %bitcast.4, s32[6,32]{1,0:T(8,128)} %bitcast.5, s32[1,32]{1,0:T(1,128)} %bitcast.7, s32[32,6]{1,0:T(8,128)} %copy.8.touch_agg, s32[1,136]{1,0:T(1,128)} %bitcast.6), custom_call_target="tpu_custom_call" | custom-call | tf_op jit(solution)/shard_map/index_tables/pallas_call | solution.py:360
  3.3 33.6 %galerkin.1.gathered = bf16[4,6,56,128]{3,2,1,0:T(8,128)(2,1)} custom-call(s32[24,128]{1,0:T(8,128)} %get-tuple-element.8.tab, bf16[32,7,192,192]{3,2,1,0:T(8,128)(2,1)} %a_ref.1, bf16[32,32,192]{2,1,0:T(8,128)(2,1)} %p_ref.1, f32[32,224]{1,0:T(8,128)} %get-tuple-element.9.ms_ref, f32[32,224]{1,0:T(8,128)} %get-tuple-element.10.ma_ref), custom_call_target="tpu_custom_call" | custom-call | tf_op jit(solution)/shard_map/galerkin/pallas_call | solution.py:371
  37.0 2.2 %index_finish.1 = f32[24,7,1024]{2,1,0:T(8,128)} custom-call(s32[24,128]{1,0:T(8,128)} %get-tuple-element.8.tab, bf16[4,6,56,128]{3,2,1,0:T(8,128)(2,1)} %galerkin.1.gathered), custom_call_target="tpu_custom_call" | custom-call | tf_op jit(solution)/shard_map/index_finish/pallas_call | solution.py:399
  39.2 2.4 %copy.9 = f32[24,7,1024]{2,0,1:T(8,128)} copy(f32[24,7,1024]{2,1,0:T(8,128)} %index_finish.1) | data formatting | bytes 1376256 | tf_op jit(solution)/shard_map/index_finish/pallas_call | solution.py:399
where the time goes:
time: 41.9 us; the launch traced here: 41.6 us
  Pallas kernels  37.8 us (90%)
  local copies, waits for them, and re-layouts  3.75 us (9%)
    pallas_call x1, Pallas kernels, on_device(): pl.pallas_call(functools.partial(kernel, n_grp, n_dev, halo, group_rows),...  33.6 us
    pallas_call x1, local copies, waits for them, and re-layouts, on_device(): pl.pallas_call(functools.partial(finish, group_rows), out_shape=jax.Shape...  2.38 us
    pallas_call x1, Pallas kernels, on_device(): pl.pallas_call(functools.partial(finish, group_rows), out_shape=jax.Shape...  2.24 us
    pallas_call x1, Pallas kernels, on_device(): pl.pallas_call(functools.partial(tables, n_grp, n_dev, halo, group_rows,...  1.96 us
    unnamed x1, local copies, waits for them, and re-layouts  1.37 us

commit v1 on v0

v1 whole, which is shorter than its diff:
```python
import functools

import jax
import jax.numpy as jnp
from jax import lax
from jax.experimental import pallas as pl
from jax.experimental.pallas import tpu as pltpu
from jax.sharding import PartitionSpec as P

EX = 4
EY = 4
MESH = pl.DeviceIdType.MESH
F32 = jnp.float32
BF16 = jnp.bfloat16


def iota(shape, dim):
    return lax.broadcasted_iota(jnp.int32, shape, dim)


def tables(
    n_grp, n_dev, halo, group_rows, rows_own,
    nbr, nbr_agg, slot, touch_agg, coarse_row,
    tab, code,
):
    grp = lax.axis_index("grp")
    dev = lax.axis_index("dev")
    device = grp * n_dev + dev
    faces, e_dev = nbr.shape
    touch, devices = touch_agg.shape
    lane = code.shape[1]
    groups = code.shape[0] // (faces + 1)
    rep = e_dev // groups

    def where_sum(mask, value, axis):
        return jnp.sum(jnp.where(mask, value, 0), axis=axis, keepdims=True)

    def put(row, value):
        tab[row:row + value.shape[0], 0:value.shape[1]] = value

    near = [
        jnp.where(grp > 0, device - n_dev, -2),
        jnp.where(grp < n_grp - 1, device + n_dev, -2),
        jnp.where(dev > 0, device - 1, -2),
        jnp.where(dev < n_dev - 1, device + 1, -2),
    ]
    ids = nbr[...]
    source = jnp.where(ids >= 0, jnp.maximum(ids, 0) // e_dev, -1)
    local = ids - source * e_dev
    hits = [jnp.max(jnp.where(source == n, 1.0, 0.0), axis=0, keepdims=True) for n in near]
    below = jnp.where(iota((e_dev, e_dev), 0) < iota((e_dev, e_dev), 1), 1.0, 0.0).astype(BF16)
    rank = jnp.dot(
        jnp.concatenate(hits + hits, axis=0).astype(BF16), below, preferred_element_type=F32
    ).astype(jnp.int32)
    lanes = iota((halo, e_dev), 1)
    for d in range(4):
        found = (rank[d:d + 1] == iota((halo, e_dev), 0)) & (hits[d] > 0)
        tab[8:8 + halo, d:d + 1] = where_sum(found, lanes, 1)
    index = iota((e_dev, e_dev), 0)
    where_from = [jnp.where(source[f:f + 1] == device, local[f:f + 1], 0) for f in range(faces)]
    for d in range(4):
        seen = jnp.zeros((e_dev, e_dev), jnp.int32)
        for f in range(faces):
            seen = jnp.where(ids[f:f + 1] == near[d] * e_dev + index, 1, seen)
        seen = jnp.max(seen, axis=1, keepdims=True)
        for f in range(faces):
            ahead = where_sum(index < local[f:f + 1], seen, 0)
            where_from[f] = jnp.where(
                source[f:f + 1] == near[d], e_dev + d * halo + ahead, where_from[f]
            )
    for f in range(faces):
        put(f, where_from[f])

    row = iota((devices, 1), 0)
    entries = touch_agg[...].T
    columns = [entries[:, t:t + 1] for t in range(touch)]
    slots = slot[...]
    put(19, slots)
    own_agg = jnp.zeros((1, e_dev), jnp.int32)
    for t in range(touch):
        own_agg = jnp.where(slots == t, where_sum(row == device, columns[t], 0), own_agg)
    valid = ids >= 0
    same = valid & (nbr_agg[...] == own_agg)
    kind = jnp.where(same, slots + touch, jnp.where(valid, slots, -1))
    kind = jnp.concatenate([slots + touch, kind], axis=0).astype(F32)
    mine = iota((groups, e_dev), 1) // rep == iota((groups, e_dev), 0)
    tall = jnp.concatenate(
        [jnp.where(mine, kind[k:k + 1], 0.0) for k in range(faces + 1)], axis=0
    ).astype(BF16)
    place = iota((e_dev, lane), 0) % rep == iota((e_dev, lane), 1) // (lane // rep)
    place = jnp.where(place, 1.0, 0.0).astype(BF16)
    code[...] = jnp.dot(tall, place, preferred_element_type=F32).astype(jnp.int32)

    n_agg = coarse_row.shape[1]
    numbers = coarse_row[...]
    across = iota((devices, n_agg), 1)
    targets = [where_sum(columns[t] == across, numbers, 1) for t in range(touch)]
    owners = [target // rows_own for target in targets]
    lane = iota((devices, rows_own), 1)
    present = jnp.zeros((devices, rows_own), F32)
    for t in range(touch):
        here = jnp.where(owners[t] == dev, targets[t] - owners[t] * rows_own, -1)
        present = jnp.where(here == lane, 1.0, present)
    mates = jnp.where(
        iota((devices, devices), 0) // n_dev == iota((devices, devices), 1) // n_dev, 1.0, 0.0
    ).astype(BF16)
    shared = jnp.dot(mates, present.astype(BF16), preferred_element_type=F32) > 0
    shared = jnp.where(shared, 1.0, 0.0)
    lower = jnp.where(
        iota((rows_own, rows_own), 0) < iota((rows_own, rows_own), 1), 1.0, 0.0
    ).astype(BF16)
    order = jnp.dot(shared.astype(BF16), lower, preferred_element_type=F32)
    heads = where_sum(row % n_dev == 0, shared * (order + 1.0 + (row // n_dev * group_rows).astype(F32)), 0)
    put(16, heads.astype(jnp.int32) - 1)
    spots = jnp.sum(present * (order + 1.0), axis=1, keepdims=True).astype(jnp.int32) - 1
    peer = iota((devices, n_dev), 1) + grp * n_dev
    put(18, where_sum(peer == iota((devices, n_dev), 0), spots, 0))
    inverse = jnp.full((1, n_dev), touch, jnp.int32)
    for t in range(touch):
        own = where_sum(row == device, owners[t], 0)
        inverse = jnp.where(own == iota((1, n_dev), 1), t, inverse)
    put(17, inverse)


def order_of(n_k):
    return list(range(1, n_k)) + [0]


def chunks_of(n_k):
    return [(p, 1) for p in range(n_k)]


def finish(tab, gathered, out_ref, flat):
    n_k, rows_own, row_width = out_ref.shape
    group_rows, sub, lane = gathered.shape[2:]

    @pl.loop(0, rows_own, unroll=4)
    def _(r):
        at = tab[16, r]
        safe = jnp.maximum(at, 0)
        for p, k in enumerate(order_of(n_k)):
            row = gathered[p, safe // group_rows, safe % group_rows].astype(F32)
            flat[k, pl.ds(pl.multiple_of(r * sub, sub), sub), :] = jnp.where(at >= 0, row, 0.0)

    for k in range(n_k):
        for j in range(sub):
            out_ref[k, :, j * lane:(j + 1) * lane] = flat[k, pl.ds(j, rows_own, stride=sub), :]


def kernel(
    n_grp, n_dev, halo, group_rows,
    tab, a_ref, p_ref, code,
    gathered,
    a_buf, pool, pack, turned, left, prod, same_sum, part_t, parts, inbox,
    a_sem, h_send, h_recv, x_send, x_recv, g_send, g_recv,
):
    grp = lax.axis_index("grp")
    dev = lax.axis_index("dev")
    e_dev, width_c, width_b = p_ref.shape
    n_k = a_ref.shape[1]
    touch, _, lane = same_sum.shape
    rep = lane // width_c
    sub = width_c // rep
    groups = e_dev // rep
    order = order_of(n_k)
    chunks = chunks_of(n_k)

    def a_copy(p):
        return pltpu.make_async_copy(a_ref.at[:, order[p]], a_buf.at[p], a_sem.at[p])

    for p in range(n_k):
        a_copy(p).start()

    barrier = pltpu.get_barrier_semaphore()
    for off in range(1, n_dev):
        pl.semaphore_signal(
            barrier, inc=1, device_id=(grp, lax.rem(dev + off, n_dev)), device_id_type=MESH
        )
    for off in range(1, n_grp):
        pl.semaphore_signal(
            barrier, inc=1, device_id=(lax.rem(grp + off, n_grp), dev), device_id_type=MESH
        )

    for j in range(4 * halo):
        pack[j] = p_ref[tab[8 + j % halo, j // halo]]
    pool[0:e_dev] = p_ref[...]
    turn = iota((width_c, width_c), 1) == iota((width_c, width_c), 0) % sub * rep + iota((width_c, width_c), 0) // sub
    turn = turn.astype(F32).astype(BF16)

    @pl.loop(0, e_dev, unroll=e_dev)
    def _(e):
        turned[e] = jnp.dot(turn, p_ref[e], preferred_element_type=F32).astype(BF16)

    same_sum[...] = jnp.zeros(same_sum.shape, F32)
    part_t[touch] = jnp.zeros(part_t.shape[1:], BF16)

    dirs = (
        (grp > 0, (grp - 1, dev)),
        (grp < n_grp - 1, (grp + 1, dev)),
        (dev > 0, (grp, dev - 1)),
        (dev < n_dev - 1, (grp, dev + 1)),
    )

    def halo_copy(d, target):
        back = d ^ 1
        return pltpu.make_async_remote_copy(
            src_ref=pack.at[pl.ds(d * halo, halo)],
            dst_ref=pool.at[pl.ds(e_dev + back * halo, halo)],
            send_sem=h_send.at[d],
            recv_sem=h_recv.at[back],
            device_id=target,
            device_id_type=MESH,
        )

    def halo_start():
        pl.semaphore_wait(barrier, n_dev + n_grp - 2)
        for d, (there, target) in enumerate(dirs):
            @pl.when(there)
            def _(d=d, target=target):
                halo_copy(d, target).start()

    def halo_wait():
        for d, (there, target) in enumerate(dirs):
            @pl.when(there)
            def _(d=d, target=target):
                halo_copy(d, target).wait_send()
                pltpu.make_async_remote_copy(
                    src_ref=pack.at[pl.ds(d * halo, halo)],
                    dst_ref=pool.at[pl.ds(e_dev + d * halo, halo)],
                    send_sem=h_send.at[d],
                    recv_sem=h_recv.at[d],
                    device_id=target,
                    device_id_type=MESH,
                ).wait_recv()

    def left_of(p):
        a_copy(p).wait()

        @pl.loop(0, e_dev, unroll=e_dev)
        def _(e):
            rows = pl.ds(pl.multiple_of(e * width_c, width_c), width_c)
            left[p, rows, :] = jnp.dot(
                turned[e], a_buf[p, e], preferred_element_type=F32
            ).astype(BF16)

    group_of_lane = iota((width_c, lane), 1) // width_c
    sub_lane = iota((sub, lane), 1) // width_c

    def squeeze(total):
        pieces = [total[j * sub:(j + 1) * sub] for j in range(rep)]
        out = None
        for s in range(rep):
            picked = pieces[s]
            for g in range(1, rep):
                picked = jnp.where(sub_lane == g, pieces[(g + s) % rep], picked)
            if s:
                picked = pltpu.roll(picked, s * width_c, 1)
            out = picked if out is None else out + picked
        return out

    def right_of(p):
        k = order[p]

        @pl.loop(0, groups, unroll=groups)
        def _(g):
            if k:
                blocks = [pool[tab[k - 1, g * rep + i]] for i in range(rep)]
            else:
                blocks = [p_ref[g * rep + i] for i in range(rep)]
            rows = pl.ds(pl.multiple_of(g * lane, lane), lane)
            full = lax.dot_general(
                left[p, rows, :], jnp.concatenate(blocks, axis=0),
                (((1,), (1,)), ((), ())), preferred_element_type=F32,
            )
            picked = full[0:width_c]
            for i in range(1, rep):
                picked = jnp.where(group_of_lane == i, full[i * width_c:(i + 1) * width_c], picked)
            prod[g] = picked

        def masked(t):
            total = None
            for g in range(groups):
                at = k * groups + g
                term = jnp.where(code[at:at + 1, :] == t, prod[g], 0.0)
                total = term if total is None else total + term
            return total

        for t in range(touch):
            same_sum[t] += masked(t + touch)
            part_t[t] = squeeze(masked(t) if k else same_sum[t]).astype(BF16)
        for o in range(n_dev):
            parts[p, o] = part_t[tab[17, o]]
        inbox[p, dev] = parts[p, dev]

    def part_copy(c, off):
        start, size = chunks[c]
        target = lax.rem(dev + off, n_dev)
        return pltpu.make_async_remote_copy(
            src_ref=parts.at[pl.ds(start, size), target],
            dst_ref=inbox.at[pl.ds(start, size), dev],
            send_sem=x_send.at[c, off],
            recv_sem=x_recv.at[c, off],
            device_id=(grp, target),
            device_id_type=MESH,
        )

    def part_arrival(c, off):
        start, size = chunks[c]
        sender = lax.rem(dev + n_dev - off, n_dev)
        return pltpu.make_async_remote_copy(
            src_ref=parts.at[pl.ds(start, size), sender],
            dst_ref=inbox.at[pl.ds(start, size), sender],
            send_sem=x_send.at[c, off],
            recv_sem=x_recv.at[c, off],
            device_id=(grp, sender),
            device_id_type=MESH,
        )

    def row_copy(c, off):
        start, size = chunks[c]
        target = lax.rem(grp + off, n_grp)
        return pltpu.make_async_remote_copy(
            src_ref=gathered.at[pl.ds(start, size), grp],
            dst_ref=gathered.at[pl.ds(start, size), grp],
            send_sem=g_send.at[c, off],
            recv_sem=g_recv.at[c, off],
            device_id=(target, dev),
            device_id_type=MESH,
        )

    def row_arrival(c, off):
        start, size = chunks[c]
        sender = lax.rem(grp + n_grp - off, n_grp)
        return pltpu.make_async_remote_copy(
            src_ref=gathered.at[pl.ds(start, size), sender],
            dst_ref=gathered.at[pl.ds(start, size), sender],
            send_sem=g_send.at[c, off],
            recv_sem=g_recv.at[c, off],
            device_id=(sender, dev),
            device_id_type=MESH,
        )

    def exchange(c):
        for off in range(1, n_dev):
            part_copy(c, off).start()

    def collect(c):
        for off in range(1, n_dev):
            part_arrival(c, off).wait_recv()
        start, size = chunks[c]
        for p in range(start, start + size):
            for j in range(group_rows):
                total = jnp.zeros((sub, lane), F32)
                for d in range(n_dev):
                    member = jnp.where(tab[18, d] == j, 1.0, 0.0).astype(F32)
                    total = total + inbox[p, d].astype(F32) * member
                gathered[p, grp, j] = total.astype(BF16)
        for off in range(1, n_grp):
            row_copy(c, off).start()

    left_of(0)
    halo_start()
    left_of(1)
    left_of(2)
    left_of(3)
    left_of(4)
    left_of(5)
    halo_wait()
    right_of(0)
    exchange(0)
    right_of(1)
    exchange(1)
    right_of(2)
    exchange(2)
    right_of(3)
    exchange(3)
    right_of(4)
    exchange(4)
    collect(0)
    right_of(5)
    exchange(5)
    collect(1)
    left_of(6)
    collect(2)
    right_of(6)
    exchange(6)
    collect(3)
    collect(4)
    collect(5)
    collect(6)

    for c in range(len(chunks)):
        for off in range(1, n_dev):
            part_copy(c, off).wait_send()
    for c in range(len(chunks)):
        for off in range(1, n_grp):
            row_arrival(c, off).wait_recv()
            row_copy(c, off).wait_send()


def on_device(n_grp, n_dev, a_blocks, prolong_t, elem_slot, touch_agg, nbr, nbr_agg, coarse_row):
    e_dev, width_c, width_b = prolong_t.shape
    n_k = a_blocks.shape[1]
    touch = touch_agg.shape[1]
    halo = e_dev // EX
    half_y = EY // 2
    span_y = half_y + 1
    group_rows = (n_dev * half_y + 1 + half_y) // span_y
    rows_own = n_grp * group_rows
    assert touch <= n_dev
    lane = 128
    rep = lane // width_c
    sub = width_c // rep
    groups = e_dev // rep
    n_chunks = len(chunks_of(n_k))
    smem = pl.BlockSpec(memory_space=pltpu.SMEM)
    vmem = pl.BlockSpec(memory_space=pltpu.VMEM)
    tab, code = pl.pallas_call(
        functools.partial(tables, n_grp, n_dev, halo, group_rows, rows_own),
        out_shape=(
            jax.ShapeDtypeStruct((24, lane), jnp.int32),
            jax.ShapeDtypeStruct((n_k * groups, lane), jnp.int32),
        ),
        in_specs=[vmem] * 5,
        out_specs=(vmem, vmem),
        name="index_tables",
    )(nbr.T, nbr_agg.T, elem_slot.reshape(1, e_dev), touch_agg.T, coarse_row.reshape(1, -1))
    gathered = pl.pallas_call(
        functools.partial(kernel, n_grp, n_dev, halo, group_rows),
        out_shape=jax.ShapeDtypeStruct((n_k, n_grp, group_rows, sub, lane), BF16),
        in_specs=[smem, pl.BlockSpec(memory_space=pl.ANY)] + [vmem] * 2,
        out_specs=vmem,
        scratch_shapes=[
            pltpu.VMEM((n_k, e_dev, width_b, width_b), BF16),
            pltpu.VMEM((e_dev + 4 * halo, width_c, width_b), BF16),
            pltpu.VMEM((4 * halo, width_c, width_b), BF16),
            pltpu.VMEM((e_dev, width_c, width_b), BF16),
            pltpu.VMEM((n_k, e_dev * width_c, width_b), BF16),
            pltpu.VMEM((groups, width_c, lane), F32),
            pltpu.VMEM((touch, width_c, lane), F32),
            pltpu.VMEM((touch + 1, sub, lane), BF16),
            pltpu.VMEM((n_k, n_dev, sub, lane), BF16),
            pltpu.VMEM((n_k, n_dev, sub, lane), BF16),
            pltpu.SemaphoreType.DMA((n_k,)),
            pltpu.SemaphoreType.DMA((4,)),
            pltpu.SemaphoreType.DMA((4,)),
            pltpu.SemaphoreType.DMA((n_chunks, n_dev)),
            pltpu.SemaphoreType.DMA((n_chunks, n_dev)),
            pltpu.SemaphoreType.DMA((n_chunks, n_grp)),
            pltpu.SemaphoreType.DMA((n_chunks, n_grp)),
        ],
        compiler_params=pltpu.CompilerParams(
            collective_id=0, has_side_effects=True, vmem_limit_bytes=60 * 1024 * 1024
        ),
        name="galerkin",
    )(tab, a_blocks, prolong_t, code)
    out = pl.pallas_call(
        finish,
        out_shape=jax.ShapeDtypeStruct((n_k, rows_own, width_c * width_c), F32),
        in_specs=[smem, vmem],
        out_specs=vmem,
        scratch_shapes=[pltpu.VMEM((n_k, rows_own * sub, lane), F32)],
        name="index_finish",
    )(tab, gathered)
    return out.transpose(1, 0, 2)


def solution(mesh):
    in_specs = (
        P(("grp", "dev"), None, None, None),
        P(("grp", "dev"), None, None),
        P(("grp", "dev")),
        P(),
        P(("grp", "dev"), None),
        P(("grp", "dev"), None),
        P(),
    )
    out_specs = P("dev", None, None)
    return jax.shard_map(
        functools.partial(on_device, mesh.shape["grp"], mesh.shape["dev"]),
        mesh=mesh, in_specs=in_specs, out_specs=out_specs, check_vma=False,
    )
```

time: 41.9 us -> 32.7 us (0.78)
  Pallas kernels: 37.8 us -> 32.3 us
  local copies, waits for them, and re-layouts: 3.75 us -> 0 us
    pallas_call x1, Pallas kernels: 33.6 us -> 28.1 us  [on_device(): pl.pallas_call(functools.partial(kernel, n_grp, n_dev, halo, group_rows),...]
    pallas_call x1 -> x0, local copies, waits for them, and re-layouts: 2.38 us -> none  [on_device(): pl.pallas_call(functools.partial(finish, group_rows), out_shape=jax.Shape...]
    unnamed x1 -> x0, local copies, waits for them, and re-layouts: 1.37 us -> none
where the time goes in v1:
time: 32.7 us; the launch traced here: 32.3 us
  Pallas kernels  32.3 us (99%)
    pallas_call x1, Pallas kernels, on_device(): pl.pallas_call(functools.partial(kernel, n_grp, n_dev, halo, group_rows),...  28.1 us
    pallas_call x1, Pallas kernels, on_device(): pl.pallas_call(finish, out_shape=jax.ShapeDtypeStruct((n_k, rows_own, wid...  2.2 us
    pallas_call x1, Pallas kernels, on_device(): pl.pallas_call(functools.partial(tables, n_grp, n_dev, halo, group_rows,...  2.03 us

profile of v1, /device:TPU:0, one launch (start us, length us, event | category | flops | bytes accessed | tf_op | source)
XLA Modules:
  0.0 32.3 jit_solution(3107567161963700046)
XLA Ops:
  0.0 2.0 %index_tables.1 = (s32[24,128]{1,0:T(8,128)}, s32[56,128]{1,0:T(8,128)}) custom-call(s32[6,32]{1,0:T(8,128)} %bitcast.6, s32[6,32]{1,0:T(8,128)} %bitcast.7, s32[1,32]{1,0:T(1,128)} %bitcast.10, s32[6,32]{1,0:T(8,128)} %bitcast.8, s32[1,136]{1,0:T(1,128)} %bitcast.9), custom_call_target="tpu_custom_call" | custom-call | tf_op jit(solution)/shard_map/index_tables/pallas_call | solution.py:418
  2.0 28.1 %galerkin.1.gathered = bf16[7,4,6,8,128]{4,3,2,1,0:T(8,128)(2,1)} custom-call(s32[24,128]{1,0:T(8,128)} %get-tuple-element.7.tab, bf16[32,7,192,192]{3,2,1,0:T(8,128)(2,1)} %a_ref.1, bf16[32,32,192]{2,1,0:T(8,128)(2,1)} %p_ref.1, s32[56,128]{1,0:T(8,128)} %get-tuple-element.8.code), custom_call_target="tpu_custom_call" | custom-call | tf_op jit(solution)/shard_map/galerkin/pallas_call | solution.py:428
  30.1 2.2 %index_finish.1 = f32[7,24,1024]{2,1,0:T(8,128)} custom-call(s32[24,128]{1,0:T(8,128)} %get-tuple-element.7.tab, bf16[7,4,6,8,128]{4,3,2,1,0:T(8,128)(2,1)} %galerkin.1.gathered), custom_call_target="tpu_custom_call" | custom-call | tf_op jit(solution)/shard_map/index_finish/pallas_call | solution.py:457

commit v2 on v1

v2 whole, which is shorter than its diff:
```python
import functools

import jax
import jax.numpy as jnp
from jax import lax
from jax.experimental import pallas as pl
from jax.experimental.pallas import tpu as pltpu
from jax.sharding import PartitionSpec as P

EX = 4
EY = 4
MESH = pl.DeviceIdType.MESH
F32 = jnp.float32
BF16 = jnp.bfloat16


def iota(shape, dim):
    return lax.broadcasted_iota(jnp.int32, shape, dim)


def where_sum(mask, value, axis):
    return jnp.sum(jnp.where(mask, value, 0), axis=axis, keepdims=True)


def ones(mask):
    return jnp.where(mask, 1.0, 0.0).astype(BF16)


def place_of(k, n_k):
    return (k + n_k - 1) % n_k


def chunks_of(n_k):
    return [(p, 1) for p in range(n_k - 2)] + [(n_k - 2, 2)]


def halo_tables(grp, dev, n_grp, n_dev, halo, nbr, tab):
    device = grp * n_dev + dev
    faces, e_dev = nbr.shape
    near = [
        jnp.where(grp > 0, device - n_dev, -2),
        jnp.where(grp < n_grp - 1, device + n_dev, -2),
        jnp.where(dev > 0, device - 1, -2),
        jnp.where(dev < n_dev - 1, device + 1, -2),
    ]
    ids = nbr
    source = jnp.where(ids >= 0, jnp.maximum(ids, 0) // e_dev, -1)
    local = ids - source * e_dev
    hits = [jnp.max(jnp.where(source == n, 1.0, 0.0), axis=0, keepdims=True) for n in near]
    below = ones(iota((e_dev, e_dev), 0) < iota((e_dev, e_dev), 1))
    rank = jnp.dot(
        jnp.concatenate(hits + hits, axis=0).astype(BF16), below, preferred_element_type=F32
    ).astype(jnp.int32)
    lanes = iota((halo, e_dev), 1)
    tab[...] = jnp.zeros(tab.shape, jnp.int32)
    for d in range(4):
        found = (rank[d:d + 1] == iota((halo, e_dev), 0)) & (hits[d] > 0)
        tab[8:8 + halo, d:d + 1] = where_sum(found, lanes, 1)
    index = iota((e_dev, e_dev), 0)
    where_from = [jnp.where(source[f:f + 1] == device, local[f:f + 1], 0) for f in range(faces)]
    for d in range(4):
        seen = jnp.zeros((e_dev, e_dev), jnp.int32)
        for f in range(faces):
            seen = jnp.where(ids[f:f + 1] == near[d] * e_dev + index, 1, seen)
        seen = jnp.max(seen, axis=1, keepdims=True)
        for f in range(faces):
            ahead = where_sum(index < local[f:f + 1], seen, 0)
            where_from[f] = jnp.where(
                source[f:f + 1] == near[d], e_dev + d * halo + ahead, where_from[f]
            )
    for f in range(faces):
        tab[f:f + 1, 0:e_dev] = where_from[f]


def owner_tables(
    grp, dev, n_dev, group_rows, rows_own,
    nbr, nbr_agg, slot, touch_agg, coarse_row, tab, code,
):
    device = grp * n_dev + dev
    faces, e_dev = nbr.shape
    touch, devices = touch_agg.shape
    lane = code.shape[1]
    groups = code.shape[0] // (faces + 1)
    rep = e_dev // groups

    def put(row, value):
        tab[row:row + 1, 0:value.shape[1]] = value

    ids = nbr
    row = iota((devices, 1), 0)
    entries = touch_agg.T
    columns = [entries[:, t:t + 1] for t in range(touch)]
    slots = slot
    own_agg = jnp.zeros((1, e_dev), jnp.int32)
    for t in range(touch):
        own_agg = jnp.where(slots == t, where_sum(row == device, columns[t], 0), own_agg)
    valid = ids >= 0
    same = valid & (nbr_agg == own_agg)
    kind = jnp.where(same, slots + touch, jnp.where(valid, slots, -1))
    kind = jnp.concatenate([slots + touch, kind], axis=0).astype(F32)
    mine = iota((groups, e_dev), 1) // rep == iota((groups, e_dev), 0)
    tall = jnp.concatenate(
        [jnp.where(mine, kind[k:k + 1], 0.0) for k in range(faces + 1)], axis=0
    ).astype(BF16)
    place = ones(iota((e_dev, lane), 0) % rep == iota((e_dev, lane), 1) // (lane // rep))
    code[...] = jnp.dot(tall, place, preferred_element_type=F32).astype(jnp.int32)

    n_agg = coarse_row.shape[1]
    numbers = coarse_row
    across = iota((devices, n_agg), 1)
    targets = [where_sum(columns[t] == across, numbers, 1) for t in range(touch)]
    owners = [target // rows_own for target in targets]
    spot = iota((devices, rows_own), 1)
    present = jnp.zeros((devices, rows_own), F32)
    for t in range(touch):
        here = jnp.where(owners[t] == dev, targets[t] - owners[t] * rows_own, -1)
        present = jnp.where(here == spot, 1.0, present)
    mates = ones(iota((devices, devices), 0) // n_dev == iota((devices, devices), 1) // n_dev)
    shared = jnp.dot(mates, present.astype(BF16), preferred_element_type=F32) > 0
    shared = jnp.where(shared, 1.0, 0.0)
    lower = ones(iota((rows_own, rows_own), 0) < iota((rows_own, rows_own), 1))
    order = jnp.dot(shared.astype(BF16), lower, preferred_element_type=F32)
    heads = where_sum(row % n_dev == 0, shared * (order + 1.0 + (row // n_dev * group_rows).astype(F32)), 0)
    tab[...] = jnp.zeros(tab.shape, jnp.int32)
    put(0, jnp.minimum(heads.astype(jnp.int32), rows_own) - 1)
    spots = jnp.sum(present * (order + 1.0), axis=1, keepdims=True).astype(jnp.int32) - 1
    peer = iota((devices, n_dev), 1) + grp * n_dev
    put(2, where_sum(peer == iota((devices, n_dev), 0), spots, 0))
    inverse = jnp.full((1, n_dev), touch, jnp.int32)
    for t in range(touch):
        own = where_sum(row == device, owners[t], 0)
        inverse = jnp.where(own == iota((1, n_dev), 1), t, inverse)
    put(1, inverse)


def kernel(
    n_grp, n_dev, halo, group_rows, rows_own, n_agg,
    a_ref, p_ref, packed,
    out_ref,
    near_v, own_v, near, own, code,
    a_buf, p_buf, pool, pack, turned, left, prod, same_sum, part_t, parts, inbox, flat,
    *rest,
):
    *gathered, a_sem, p_sem, t_sem, h_send, h_recv, x_send, x_recv, g_send, g_recv = rest
    grp = lax.axis_index("grp")
    dev = lax.axis_index("dev")
    e_dev, width_c, width_b = p_ref.shape
    n_k = a_ref.shape[1]
    touch, _, lane = same_sum.shape
    rep = lane // width_c
    sub = width_c // rep
    groups = e_dev // rep
    chunks = chunks_of(n_k)
    parted = a_sem.shape[1]

    def a_copies(k):
        count = parted if k == 0 else 1
        size = e_dev // count
        return [
            pltpu.make_async_copy(
                a_ref.at[pl.ds(q * size, size), k], a_buf.at[k, pl.ds(q * size, size)], a_sem.at[k, q]
            )
            for q in range(count)
        ]

    faces = n_k - 1
    nbr = packed[0:faces, 0:e_dev]
    nbr_agg = packed[8:8 + faces, 0:e_dev]
    touch_agg = packed[16:16 + touch, 0:n_grp * n_dev]
    slot = packed[24:25, 0:e_dev]
    coarse_row = packed[32:33, 0:n_agg]
    p_copy = pltpu.make_async_copy(p_ref, p_buf, p_sem.at[0])
    near_copy = pltpu.make_async_copy(near_v, near, t_sem.at[0])
    own_copy = pltpu.make_async_copy(own_v, own, t_sem.at[1])
    p_copy.start()

    barrier = pltpu.get_barrier_semaphore()
    for off in range(1, n_dev):
        pl.semaphore_signal(
            barrier, inc=1, device_id=(grp, lax.rem(dev + off, n_dev)), device_id_type=MESH
        )
    for off in range(1, n_grp):
        pl.semaphore_signal(
            barrier, inc=1, device_id=(lax.rem(grp + off, n_grp), dev), device_id_type=MESH
        )

    dirs = (
        (grp > 0, (grp - 1, dev)),
        (grp < n_grp - 1, (grp + 1, dev)),
        (dev > 0, (grp, dev - 1)),
        (dev < n_dev - 1, (grp, dev + 1)),
    )

    def halo_copy(d, target):
        back = d ^ 1
        return pltpu.make_async_remote_copy(
            src_ref=pack.at[pl.ds(d * halo, halo)],
            dst_ref=pool.at[pl.ds(e_dev + back * halo, halo)],
            send_sem=h_send.at[d],
            recv_sem=h_recv.at[back],
            device_id=target,
            device_id_type=MESH,
        )

    def tables_one():
        halo_tables(grp, dev, n_grp, n_dev, halo, nbr, near_v)
        near_copy.start()

    def tables_two():
        owner_tables(
            grp, dev, n_dev, group_rows, rows_own,
            nbr, nbr_agg, slot, touch_agg, coarse_row, own_v, code,
        )
        part_t[touch] = jnp.zeros(part_t.shape[1:], BF16)
        own_copy.start()

    def a_first():
        for copy in a_copies(0):
            copy.start()

    def p_wait():
        p_copy.wait()
        for k in range(1, n_k):
            for copy in a_copies(k):
                copy.start()

    def turn_p():
        turn = ones(
            iota((width_c, width_c), 1)
            == iota((width_c, width_c), 0) % sub * rep + iota((width_c, width_c), 0) // sub
        )

        @pl.loop(0, e_dev, unroll=e_dev)
        def _(e):
            turned[e] = jnp.dot(turn, p_buf[e], preferred_element_type=F32).astype(BF16)

    def halo_start():
        near_copy.wait()
        for j in range(4 * halo):
            pack[j] = p_buf[near[8 + j % halo, j // halo]]
        pool[0:e_dev] = p_buf[...]
        pl.semaphore_wait(barrier, n_dev + n_grp - 2)
        for d, (there, target) in enumerate(dirs):
            @pl.when(there)
            def _(d=d, target=target):
                halo_copy(d, target).start()

    def halo_wait():
        for d, (there, target) in enumerate(dirs):
            @pl.when(there)
            def _(d=d, target=target):
                halo_copy(d, target).wait_send()
                pltpu.make_async_remote_copy(
                    src_ref=pack.at[pl.ds(d * halo, halo)],
                    dst_ref=pool.at[pl.ds(e_dev + d * halo, halo)],
                    send_sem=h_send.at[d],
                    recv_sem=h_recv.at[d],
                    device_id=target,
                    device_id_type=MESH,
                ).wait_recv()

    def left_of(k):
        copies = a_copies(k)
        for q, copy in enumerate(copies):
            copy.wait()
            size = e_dev // len(copies)

            @pl.loop(q * size, (q + 1) * size, unroll=size)
            def _(e):
                rows = pl.ds(pl.multiple_of(e * width_c, width_c), width_c)
                left[k, rows, :] = jnp.dot(
                    turned[e], a_buf[k, e], preferred_element_type=F32
                ).astype(BF16)

    group_of_lane = iota((width_c, lane), 1) // width_c
    sub_lane = iota((sub, lane), 1) // width_c

    def squeeze(total):
        pieces = [total[j * sub:(j + 1) * sub] for j in range(rep)]
        out = None
        for s in range(rep):
            picked = pieces[s]
            for g in range(1, rep):
                picked = jnp.where(sub_lane == g, pieces[(g + s) % rep], picked)
            if s:
                picked = pltpu.roll(picked, s * width_c, 1)
            out = picked if out is None else out + picked
        return out

    def right_of(k):
        @pl.loop(0, groups, unroll=groups)
        def _(g):
            if k:
                blocks = [pool[near[k - 1, g * rep + i]] for i in range(rep)]
            else:
                blocks = [p_buf[g * rep + i] for i in range(rep)]
            rows = pl.ds(pl.multiple_of(g * lane, lane), lane)
            full = lax.dot_general(
                left[k, rows, :], jnp.concatenate(blocks, axis=0),
                (((1,), (1,)), ((), ())), preferred_element_type=F32,
            )
            picked = full[0:width_c]
            for i in range(1, rep):
                picked = jnp.where(group_of_lane == i, full[i * width_c:(i + 1) * width_c], picked)
            prod[k % 2, g] = picked

        def masked(t):
            total = None
            for g in range(groups):
                at = k * groups + g
                term = jnp.where(code[at:at + 1, :] == t, prod[k % 2, g], 0.0)
                total = term if total is None else total + term
            return total

        for t in range(touch):
            together = masked(t + touch)
            if k:
                together = same_sum[t] + together
            same_sum[t] = together
            if k:
                part_t[t] = squeeze(masked(t)).astype(BF16)
        if k:
            emit(k)
        if k == n_k - 1:
            for t in range(touch):
                part_t[t] = squeeze(same_sum[t]).astype(BF16)
            emit(0)

    def emit(k):
        p = place_of(k, n_k)
        for o in range(n_dev):
            parts[p, o] = part_t[own[1, o]]
        inbox[p, dev] = parts[p, dev]

    def part_copy(c, off):
        start, size = chunks[c]
        target = lax.rem(dev + off, n_dev)
        return pltpu.make_async_remote_copy(
            src_ref=parts.at[pl.ds(start, size), target],
            dst_ref=inbox.at[pl.ds(start, size), dev],
            send_sem=x_send.at[c, off],
            recv_sem=x_recv.at[c, off],
            device_id=(grp, target),
            device_id_type=MESH,
        )

    def part_arrival(c, off):
        start, size = chunks[c]
        sender = lax.rem(dev + n_dev - off, n_dev)
        return pltpu.make_async_remote_copy(
            src_ref=parts.at[pl.ds(start, size), sender],
            dst_ref=inbox.at[pl.ds(start, size), sender],
            send_sem=x_send.at[c, off],
            recv_sem=x_recv.at[c, off],
            device_id=(grp, sender),
            device_id_type=MESH,
        )

    def row_copy(c, off):
        target = lax.rem(grp + off, n_grp)
        return pltpu.make_async_remote_copy(
            src_ref=gathered[c].at[pl.ds(grp * group_rows, group_rows)],
            dst_ref=gathered[c].at[pl.ds(grp * group_rows, group_rows)],
            send_sem=g_send.at[c, off],
            recv_sem=g_recv.at[c, off],
            device_id=(target, dev),
            device_id_type=MESH,
        )

    def row_arrival(c, off):
        sender = lax.rem(grp + n_grp - off, n_grp)
        return pltpu.make_async_remote_copy(
            src_ref=gathered[c].at[pl.ds(sender * group_rows, group_rows)],
            dst_ref=gathered[c].at[pl.ds(sender * group_rows, group_rows)],
            send_sem=g_send.at[c, off],
            recv_sem=g_recv.at[c, off],
            device_id=(sender, dev),
            device_id_type=MESH,
        )

    def exchange(c):
        for off in range(1, n_dev):
            part_copy(c, off).start()

    def collect(c):
        for off in range(1, n_dev):
            part_arrival(c, off).wait_recv()
        start, size = chunks[c]
        for j in range(group_rows):
            for i in range(size):
                total = jnp.zeros((sub, lane), F32)
                for d in range(n_dev):
                    member = jnp.where(own[2, d] == j, 1.0, 0.0).astype(F32)
                    total = total + inbox[start + i, d].astype(F32) * member
                gathered[c][grp * group_rows + j, i] = total.astype(BF16)
        for off in range(1, n_grp):
            row_copy(c, off).start()

    def place(c):
        for off in range(1, n_grp):
            row_arrival(c, off).wait_recv()
        start, size = chunks[c]
        for i in range(size):
            k = (start + i + 1) % n_k

            @pl.loop(0, rows_own, unroll=8)
            def _(r, i=i):
                at = own[0, r]
                row = gathered[c][jnp.maximum(at, 0), i].astype(F32)
                flat[i, pl.ds(pl.multiple_of(r * sub, sub), sub), :] = jnp.where(at >= 0, row, 0.0)

            for j in range(sub):
                out_ref[k, :, j * lane:(j + 1) * lane] = flat[i, pl.ds(j, rows_own, stride=sub), :].astype(BF16)

    def sent():
        for c in range(len(chunks)):
            for off in range(1, n_dev):
                part_copy(c, off).wait_send()
            for off in range(1, n_grp):
                row_copy(c, off).wait_send()

    tables_one()
    a_first()
    tables_two()
    p_wait()
    halo_start()
    turn_p()
    left_of(0)
    own_copy.wait()
    right_of(0)
    left_of(1)
    left_of(2)
    halo_wait()
    right_of(1)
    exchange(0)
    left_of(3)
    right_of(2)
    exchange(1)
    left_of(4)
    right_of(3)
    exchange(2)
    left_of(5)
    right_of(4)
    exchange(3)
    collect(0)
    left_of(6)
    right_of(5)
    exchange(4)
    collect(1)
    right_of(6)
    exchange(5)
    collect(2)
    collect(3)
    collect(4)
    place(0)
    place(1)
    collect(5)
    place(2)
    place(3)
    place(4)
    place(5)
    sent()


def on_device(n_grp, n_dev, a_blocks, prolong_t, elem_slot, touch_agg, nbr, nbr_agg, coarse_row):
    e_dev, width_c, width_b = prolong_t.shape
    n_k = a_blocks.shape[1]
    touch = touch_agg.shape[1]
    halo = e_dev // EX
    half_y = EY // 2
    span_y = half_y + 1
    group_rows = (n_dev * half_y + 1 + half_y) // span_y
    rows_own = n_grp * group_rows
    assert touch <= n_dev
    lane = 128
    rep = lane // width_c
    sub = width_c // rep
    groups = e_dev // rep
    chunks = chunks_of(n_k)
    n_chunks = len(chunks)
    parted = 2
    hbm = pl.BlockSpec(memory_space=pltpu.HBM)
    vmem = pl.BlockSpec(memory_space=pltpu.VMEM)
    ints = [nbr.T, nbr_agg.T, touch_agg.T, elem_slot.reshape(1, e_dev), coarse_row.reshape(1, -1)]
    width = -(-max(x.shape[1] for x in ints) // lane) * lane
    packed = sum(
        jnp.pad(x, ((8 * i, 8 * (len(ints) - i) - x.shape[0]), (0, width - x.shape[1])))
        for i, x in enumerate(ints)
    )
    out = pl.pallas_call(
        functools.partial(kernel, n_grp, n_dev, halo, group_rows, rows_own, coarse_row.shape[0]),
        out_shape=jax.ShapeDtypeStruct((n_k, rows_own, width_c * width_c), BF16),
        in_specs=[hbm] * 2 + [vmem],
        out_specs=vmem,
        scratch_shapes=[
            pltpu.VMEM((16, lane), jnp.int32),
            pltpu.VMEM((8, lane), jnp.int32),
            pltpu.SMEM((16, lane), jnp.int32),
            pltpu.SMEM((8, lane), jnp.int32),
            pltpu.VMEM((n_k * groups, lane), jnp.int32),
            pltpu.VMEM((n_k, e_dev, width_b, width_b), BF16),
            pltpu.VMEM((e_dev, width_c, width_b), BF16),
            pltpu.VMEM((e_dev + 4 * halo, width_c, width_b), BF16),
            pltpu.VMEM((4 * halo, width_c, width_b), BF16),
            pltpu.VMEM((e_dev, width_c, width_b), BF16),
            pltpu.VMEM((n_k, e_dev * width_c, width_b), BF16),
            pltpu.VMEM((2, groups, width_c, lane), F32),
            pltpu.VMEM((touch, width_c, lane), F32),
            pltpu.VMEM((touch + 1, sub, lane), BF16),
            pltpu.VMEM((n_k, n_dev, sub, lane), BF16),
            pltpu.VMEM((n_k, n_dev, sub, lane), BF16),
            pltpu.VMEM((2, rows_own * sub, lane), F32),
        ] + [pltpu.VMEM((rows_own, size, sub, lane), BF16) for _, size in chunks] + [
            pltpu.SemaphoreType.DMA((n_k, parted)),
            pltpu.SemaphoreType.DMA((1,)),
            pltpu.SemaphoreType.DMA((2,)),
            pltpu.SemaphoreType.DMA((4,)),
            pltpu.SemaphoreType.DMA((4,)),
            pltpu.SemaphoreType.DMA((n_chunks, n_dev)),
            pltpu.SemaphoreType.DMA((n_chunks, n_dev)),
            pltpu.SemaphoreType.DMA((n_chunks, n_grp)),
            pltpu.SemaphoreType.DMA((n_chunks, n_grp)),
        ],
        compiler_params=pltpu.CompilerParams(
            collective_id=0, has_side_effects=True, vmem_limit_bytes=54656 * 1024
        ),
        name="galerkin",
    )(a_blocks, prolong_t, packed)
    return out.astype(F32).transpose(1, 0, 2)


def solution(mesh):
    in_specs = (
        P(("grp", "dev"), None, None, None),
        P(("grp", "dev"), None, None),
        P(("grp", "dev")),
        P(),
        P(("grp", "dev"), None),
        P(("grp", "dev"), None),
        P(),
    )
    out_specs = P("dev", None, None)
    return jax.shard_map(
        functools.partial(on_device, mesh.shape["grp"], mesh.shape["dev"]),
        mesh=mesh, in_specs=in_specs, out_specs=out_specs, check_vma=False,
    )
```

time: 32.7 us -> 27.2 us (0.83)
  Pallas kernels: 32.3 us -> 25.4 us
  other arithmetic: 0 us -> 1.67 us
    pallas_call x3 -> x1, Pallas kernels: 32.3 us -> 25.4 us  [on_device(): pl.pallas_call(functools.partial(kernel, n_grp, n_dev, halo, group_rows,...]
    transpose x0 -> x1, other arithmetic: none -> 0.92 us  [on_device(): return out.astype(F32).transpose(1, 0, 2)]
    add x0 -> x1, other arithmetic: none -> 0.76 us  [on_device(): sum((jnp.pad(x, ((8 * i, 8 * (len(ints) - i) - x.shape[0]), (0, width - x...]
where the time goes in v2:
time: 27.2 us; the launch traced here: 27.1 us
  Pallas kernels  25.4 us (93%)
  other arithmetic  1.67 us (6%)
    pallas_call x1, Pallas kernels, on_device(): pl.pallas_call(functools.partial(kernel, n_grp, n_dev, halo, group_rows,...  25.4 us
    transpose x1, other arithmetic, on_device(): return out.astype(F32).transpose(1, 0, 2)  0.92 us
    add x1, other arithmetic, on_device(): sum((jnp.pad(x, ((8 * i, 8 * (len(ints) - i) - x.shape[0]), (0, width - x...  0.76 us

profile of v2, /device:TPU:0, one launch (start us, length us, event | category | flops | bytes accessed | tf_op | source)
XLA Modules:
  0.0 27.1 jit_solution(16341419487013555010)
XLA Ops:
  0.0 0.8 %pad_add_fusion.packed = s32[40,256]{1,0:T(8,128)S(1)} fusion(s32[1,136]{1,0:T(1,128)} %bitcast.10, s32[1,32]{1,0:T(1,128)} %bitcast.11, s32[6,32]{1,0:T(8,128)} %bitcast.7, s32[6,32]{1,0:T(8,128)} %bitcast.8, s32[6,32]{1,0:T(8,128)} %bitcast.9), kind=kLoop, calls=%fused_computation.1 | loop fusion | flops 40960 | bytes 43936 | tf_op jit(solution)/shard_map/add | solution.py:486
  0.8 25.4 %galerkin.1 = bf16[7,24,1024]{2,1,0:T(8,128)(2,1)S(1)} custom-call(bf16[32,7,192,192]{3,2,1,0:T(8,128)(2,1)} %a_ref.1, bf16[32,32,192]{2,1,0:T(8,128)(2,1)} %p_ref.1, s32[40,256]{1,0:T(8,128)S(1)} %pad_add_fusion.packed), custom_call_target="tpu_custom_call" | custom-call | tf_op jit(solution)/shard_map/galerkin/pallas_call | solution.py:490
  26.1 0.9 %convert_bitcast_fusion = f32[24,7,1024]{2,0,1:T(8,128)} fusion(bf16[7,24,1024]{2,1,0:T(8,128)(2,1)S(1)} %galerkin.1), kind=kLoop, calls=%fused_computation | loop fusion | flops 172032 | bytes 1032192 | tf_op jit(solution)/shard_map/transpose | solution.py:529

commit v3 on v2

--- a/solution.py
+++ b/solution.py
@@ -31,7 +31,7 @@
 
 
 def chunks_of(n_k):
-    return [(p, 1) for p in range(n_k - 2)] + [(n_k - 2, 2)]
+    return [(p, 1) for p in range(n_k)]
 
 
 def halo_tables(grp, dev, n_grp, n_dev, halo, nbr, tab):
@@ -151,14 +151,14 @@
     sub = width_c // rep
     groups = e_dev // rep
     chunks = chunks_of(n_k)
-    parted = a_sem.shape[1]
+    parted = a_sem.shape[0] - n_k + 1
 
     def a_copies(k):
-        count = parted if k == 0 else 1
+        count = parted if k == 1 else 1
         size = e_dev // count
         return [
             pltpu.make_async_copy(
-                a_ref.at[pl.ds(q * size, size), k], a_buf.at[k, pl.ds(q * size, size)], a_sem.at[k, q]
+                a_ref.at[pl.ds(q * size, size), k], a_buf.at[k, pl.ds(q * size, size)], a_sem.at[place_of(k, n_k) + (q if k == 1 else parted - 1)]
             )
             for q in range(count)
         ]
@@ -215,12 +215,12 @@
         own_copy.start()
 
     def a_first():
-        for copy in a_copies(0):
+        for copy in a_copies(1):
             copy.start()
 
     def p_wait():
         p_copy.wait()
-        for k in range(1, n_k):
+        for k in list(range(2, n_k)) + [0]:
             for copy in a_copies(k):
                 copy.start()
 
@@ -287,7 +287,7 @@
             out = picked if out is None else out + picked
         return out
 
-    def right_of(k):
+    def right_mm(k):
         @pl.loop(0, groups, unroll=groups)
         def _(g):
             if k:
@@ -304,6 +304,7 @@
                 picked = jnp.where(group_of_lane == i, full[i * width_c:(i + 1) * width_c], picked)
             prod[k % 2, g] = picked
 
+    def right_sum(k):
         def masked(t):
             total = None
             for g in range(groups):
@@ -314,19 +315,11 @@
 
         for t in range(touch):
             together = masked(t + touch)
+            if k != 1:
+                together = same_sum[t] + together
             if k:
-                together = same_sum[t] + together
-            same_sum[t] = together
-            if k:
-                part_t[t] = squeeze(masked(t)).astype(BF16)
-        if k:
-            emit(k)
-        if k == n_k - 1:
-            for t in range(touch):
-                part_t[t] = squeeze(same_sum[t]).astype(BF16)
-            emit(0)
-
-    def emit(k):
+                same_sum[t] = together
+            part_t[t] = squeeze(masked(t) if k else together).astype(BF16)
         p = place_of(k, n_k)
         for o in range(n_dev):
             parts[p, o] = part_t[own[1, o]]
@@ -338,21 +331,20 @@
         return pltpu.make_async_remote_copy(
             src_ref=parts.at[pl.ds(start, size), target],
             dst_ref=inbox.at[pl.ds(start, size), dev],
-            send_sem=x_send.at[c, off],
-            recv_sem=x_recv.at[c, off],
+            send_sem=x_send.at[c],
+            recv_sem=x_recv.at[c],
             device_id=(grp, target),
             device_id_type=MESH,
         )
 
-    def part_arrival(c, off):
+    def part_all(c):
         start, size = chunks[c]
-        sender = lax.rem(dev + n_dev - off, n_dev)
         return pltpu.make_async_remote_copy(
-            src_ref=parts.at[pl.ds(start, size), sender],
-            dst_ref=inbox.at[pl.ds(start, size), sender],
-            send_sem=x_send.at[c, off],
-            recv_sem=x_recv.at[c, off],
-            device_id=(grp, sender),
+            src_ref=parts.at[pl.ds(start, size), pl.ds(0, n_dev - 1)],
+            dst_ref=inbox.at[pl.ds(start, size), pl.ds(0, n_dev - 1)],
+            send_sem=x_send.at[c],
+            recv_sem=x_recv.at[c],
+            device_id=(grp, lax.rem(dev + 1, n_dev)),
             device_id_type=MESH,
         )
 
@@ -361,20 +353,19 @@
         return pltpu.make_async_remote_copy(
             src_ref=gathered[c].at[pl.ds(grp * group_rows, group_rows)],
             dst_ref=gathered[c].at[pl.ds(grp * group_rows, group_rows)],
-            send_sem=g_send.at[c, off],
-            recv_sem=g_recv.at[c, off],
+            send_sem=g_send.at[c],
+            recv_sem=g_recv.at[c],
             device_id=(target, dev),
             device_id_type=MESH,
         )
 
-    def row_arrival(c, off):
-        sender = lax.rem(grp + n_grp - off, n_grp)
+    def row_all(c):
         return pltpu.make_async_remote_copy(
-            src_ref=gathered[c].at[pl.ds(sender * group_rows, group_rows)],
-            dst_ref=gathered[c].at[pl.ds(sender * group_rows, group_rows)],
-            send_sem=g_send.at[c, off],
-            recv_sem=g_recv.at[c, off],
-            device_id=(sender, dev),
+            src_ref=gathered[c].at[pl.ds(0, (n_grp - 1) * group_rows)],
+            dst_ref=gathered[c].at[pl.ds(0, (n_grp - 1) * group_rows)],
+            send_sem=g_send.at[c],
+            recv_sem=g_recv.at[c],
+            device_id=(lax.rem(grp + 1, n_grp), dev),
             device_id_type=MESH,
         )
 
@@ -383,8 +374,7 @@
             part_copy(c, off).start()
 
     def collect(c):
-        for off in range(1, n_dev):
-            part_arrival(c, off).wait_recv()
+        part_all(c).wait_recv()
         start, size = chunks[c]
         for j in range(group_rows):
             for i in range(size):
@@ -396,28 +386,26 @@
         for off in range(1, n_grp):
             row_copy(c, off).start()
 
+    def put_rows(rows, i, k):
+        @pl.loop(0, rows_own, unroll=8)
+        def _(r):
+            at = own[0, r]
+            row = rows[jnp.maximum(at, 0), i].astype(F32)
+            flat[pl.ds(pl.multiple_of(r * sub, sub), sub), :] = jnp.where(at >= 0, row, 0.0)
+
+        for j in range(sub):
+            out_ref[k, :, j * lane:(j + 1) * lane] = flat[pl.ds(j, rows_own, stride=sub), :].astype(BF16)
+
     def place(c):
-        for off in range(1, n_grp):
-            row_arrival(c, off).wait_recv()
+        row_all(c).wait_recv()
         start, size = chunks[c]
         for i in range(size):
-            k = (start + i + 1) % n_k
-
-            @pl.loop(0, rows_own, unroll=8)
-            def _(r, i=i):
-                at = own[0, r]
-                row = gathered[c][jnp.maximum(at, 0), i].astype(F32)
-                flat[i, pl.ds(pl.multiple_of(r * sub, sub), sub), :] = jnp.where(at >= 0, row, 0.0)
-
-            for j in range(sub):
-                out_ref[k, :, j * lane:(j + 1) * lane] = flat[i, pl.ds(j, rows_own, stride=sub), :].astype(BF16)
+            put_rows(gathered[c], i, (start + i + 1) % n_k)
 
     def sent():
         for c in range(len(chunks)):
-            for off in range(1, n_dev):
-                part_copy(c, off).wait_send()
-            for off in range(1, n_grp):
-                row_copy(c, off).wait_send()
+            part_all(c).wait_send()
+            row_all(c).wait_send()
 
     tables_one()
     a_first()
@@ -425,40 +413,50 @@
     p_wait()
     halo_start()
     turn_p()
-    left_of(0)
-    own_copy.wait()
-    right_of(0)
     left_of(1)
     left_of(2)
+    own_copy.wait()
+    left_of(3)
+    left_of(4)
     halo_wait()
-    right_of(1)
+    right_mm(1)
+    right_sum(1)
     exchange(0)
-    left_of(3)
-    right_of(2)
+    right_mm(2)
+    right_sum(2)
     exchange(1)
-    left_of(4)
-    right_of(3)
+    left_of(5)
+    right_mm(3)
+    right_sum(3)
     exchange(2)
-    left_of(5)
-    right_of(4)
+    left_of(6)
+    right_mm(4)
+    right_sum(4)
     exchange(3)
+    right_mm(5)
+    right_sum(5)
+    exchange(4)
     collect(0)
-    left_of(6)
-    right_of(5)
-    exchange(4)
+    right_mm(6)
+    right_sum(6)
+    exchange(5)
     collect(1)
-    right_of(6)
-    exchange(5)
+    left_of(0)
+    right_mm(0)
+    right_sum(0)
+    exchange(6)
     collect(2)
     collect(3)
     collect(4)
+    collect(5)
+    collect(6)
     place(0)
     place(1)
-    collect(5)
     place(2)
     place(3)
     place(4)
     place(5)
+    place(6)
     sent()
 
 
@@ -509,17 +507,17 @@
             pltpu.VMEM((touch + 1, sub, lane), BF16),
             pltpu.VMEM((n_k, n_dev, sub, lane), BF16),
             pltpu.VMEM((n_k, n_dev, sub, lane), BF16),
-            pltpu.VMEM((2, rows_own * sub, lane), F32),
+            pltpu.VMEM((rows_own * sub, lane), F32),
         ] + [pltpu.VMEM((rows_own, size, sub, lane), BF16) for _, size in chunks] + [
-            pltpu.SemaphoreType.DMA((n_k, parted)),
+            pltpu.SemaphoreType.DMA((n_k + parted - 1,)),
             pltpu.SemaphoreType.DMA((1,)),
             pltpu.SemaphoreType.DMA((2,)),
             pltpu.SemaphoreType.DMA((4,)),
             pltpu.SemaphoreType.DMA((4,)),
-            pltpu.SemaphoreType.DMA((n_chunks, n_dev)),
-            pltpu.SemaphoreType.DMA((n_chunks, n_dev)),
-            pltpu.SemaphoreType.DMA((n_chunks, n_grp)),
-            pltpu.SemaphoreType.DMA((n_chunks, n_grp)),
+            pltpu.SemaphoreType.DMA((n_chunks,)),
+            pltpu.SemaphoreType.DMA((n_chunks,)),
+            pltpu.SemaphoreType.DMA((n_chunks,)),
+            pltpu.SemaphoreType.DMA((n_chunks,)),
         ],
         compiler_params=pltpu.CompilerParams(
             collective_id=0, has_side_effects=True, vmem_limit_bytes=54656 * 1024

time: 27.2 us -> 25.8 us (0.949)
  Pallas kernels: 25.4 us -> 24 us
    pallas_call x1, Pallas kernels: 25.4 us -> 24 us  [on_device(): pl.pallas_call(functools.partial(kernel, n_grp, n_dev, halo, group_rows,...]
where the time goes in v3:
time: 25.8 us; the launch traced here: 25.7 us
  Pallas kernels  24 us (93%)
  other arithmetic  1.67 us (6%)
    pallas_call x1, Pallas kernels, on_device(): pl.pallas_call(functools.partial(kernel, n_grp, n_dev, halo, group_rows,...  24 us
    transpose x1, other arithmetic, on_device(): return out.astype(F32).transpose(1, 0, 2)  0.92 us
    add x1, other arithmetic, on_device(): sum((jnp.pad(x, ((8 * i, 8 * (len(ints) - i) - x.shape[0]), (0, width - x...  0.76 us

profile of v3, /device:TPU:0, one launch (start us, length us, event | category | flops | bytes accessed | tf_op | source)
XLA Modules:
  0.0 25.7 jit_solution(10687087571788802556)
XLA Ops:
  0.0 0.8 %pad_add_fusion.packed = s32[40,256]{1,0:T(8,128)S(1)} fusion(s32[1,136]{1,0:T(1,128)} %bitcast.10, s32[1,32]{1,0:T(1,128)} %bitcast.11, s32[6,32]{1,0:T(8,128)} %bitcast.7, s32[6,32]{1,0:T(8,128)} %bitcast.8, s32[6,32]{1,0:T(8,128)} %bitcast.9), kind=kLoop, calls=%fused_computation.1 | loop fusion | flops 40960 | bytes 43936 | tf_op jit(solution)/shard_map/add | solution.py:484
  0.8 24.0 %galerkin.1 = bf16[7,24,1024]{2,1,0:T(8,128)(2,1)S(1)} custom-call(bf16[32,7,192,192]{3,2,1,0:T(8,128)(2,1)} %a_ref.1, bf16[32,32,192]{2,1,0:T(8,128)(2,1)} %p_ref.1, s32[40,256]{1,0:T(8,128)S(1)} %pad_add_fusion.packed), custom_call_target="tpu_custom_call" | custom-call | tf_op jit(solution)/shard_map/galerkin/pallas_call | solution.py:488
  24.7 0.9 %convert_bitcast_fusion = f32[24,7,1024]{2,0,1:T(8,128)} fusion(bf16[7,24,1024]{2,1,0:T(8,128)(2,1)S(1)} %galerkin.1), kind=kLoop, calls=%fused_computation | loop fusion | flops 172032 | bytes 1032192 | tf_op jit(solution)/shard_map/transpose | solution.py:527

commit v4 on v3

--- a/solution.py
+++ b/solution.py
@@ -30,8 +30,12 @@
     return (k + n_k - 1) % n_k
 
 
+def early_of(n_k):
+    return 2
+
+
 def chunks_of(n_k):
-    return [(p, 1) for p in range(n_k)]
+    return [(p, 2) for p in range(early_of(n_k), n_k - 1, 2)] + [(n_k - 1, 1)]
 
 
 def halo_tables(grp, dev, n_grp, n_dev, halo, nbr, tab):
@@ -74,7 +78,7 @@
 
 def owner_tables(
     grp, dev, n_dev, group_rows, rows_own,
-    nbr, nbr_agg, slot, touch_agg, coarse_row, tab, code,
+    nbr, nbr_agg, slot, touch_agg, coarse_row, tab, code, spot_of,
 ):
     device = grp * n_dev + dev
     faces, e_dev = nbr.shape
@@ -124,6 +128,7 @@
     tab[...] = jnp.zeros(tab.shape, jnp.int32)
     put(0, jnp.minimum(heads.astype(jnp.int32), rows_own) - 1)
     spots = jnp.sum(present * (order + 1.0), axis=1, keepdims=True).astype(jnp.int32) - 1
+    spot_of[...] = jnp.broadcast_to(spots, spot_of.shape)
     peer = iota((devices, n_dev), 1) + grp * n_dev
     put(2, where_sum(peer == iota((devices, n_dev), 0), spots, 0))
     inverse = jnp.full((1, n_dev), touch, jnp.int32)
@@ -138,10 +143,10 @@
     a_ref, p_ref, packed,
     out_ref,
     near_v, own_v, near, own, code,
-    a_buf, p_buf, pool, pack, turned, left, prod, same_sum, part_t, parts, inbox, flat,
+    a_buf, p_buf, pool, tail, pack, tail_pack, tail_in, turned, left, prod, same_sum, part_t, parts, inbox, flat, spot_of, z_in, y_in, early_rows,
     *rest,
 ):
-    *gathered, a_sem, p_sem, t_sem, h_send, h_recv, x_send, x_recv, g_send, g_recv = rest
+    *gathered, a_sem, p_sem, t_sem, h_send, h_recv, x_send, x_recv, g_send, g_recv, f_recv, z_sem, y_sem = rest
     grp = lax.axis_index("grp")
     dev = lax.axis_index("dev")
     e_dev, width_c, width_b = p_ref.shape
@@ -151,6 +156,8 @@
     sub = width_c // rep
     groups = e_dev // rep
     chunks = chunks_of(n_k)
+    early = early_of(n_k)
+    rest_b = width_b - lane
     parted = a_sem.shape[0] - n_k + 1
 
     def a_copies(k):
@@ -191,13 +198,13 @@
         (dev < n_dev - 1, (grp, dev + 1)),
     )
 
-    def halo_copy(d, target):
-        back = d ^ 1
-        return pltpu.make_async_remote_copy(
-            src_ref=pack.at[pl.ds(d * halo, halo)],
-            dst_ref=pool.at[pl.ds(e_dev + back * halo, halo)],
-            send_sem=h_send.at[d],
-            recv_sem=h_recv.at[back],
+    def halo_copy(part, d, target, back):
+        source, sink, base, size = ((pack, pool, e_dev, halo), (tail_pack, tail_in, 0, halo // 2))[part]
+        return pltpu.make_async_remote_copy(
+            src_ref=source.at[pl.ds(d * size, size)],
+            dst_ref=sink.at[pl.ds(base + back * size, size)],
+            send_sem=h_send.at[4 * part + d],
+            recv_sem=h_recv.at[4 * part + back],
             device_id=target,
             device_id_type=MESH,
         )
@@ -209,7 +216,7 @@
     def tables_two():
         owner_tables(
             grp, dev, n_dev, group_rows, rows_own,
-            nbr, nbr_agg, slot, touch_agg, coarse_row, own_v, code,
+            nbr, nbr_agg, slot, touch_agg, coarse_row, own_v, code, spot_of,
         )
         part_t[touch] = jnp.zeros(part_t.shape[1:], BF16)
         own_copy.start()
@@ -236,41 +243,48 @@
 
     def halo_start():
         near_copy.wait()
+        def start(part):
+            for d, (there, target) in enumerate(dirs):
+                @pl.when(there)
+                def _(d=d, target=target):
+                    halo_copy(part, d, target, d ^ 1).start()
+
         for j in range(4 * halo):
-            pack[j] = p_buf[near[8 + j % halo, j // halo]]
-        pool[0:e_dev] = p_buf[...]
+            pack[j] = p_buf[near[8 + j % halo, j // halo], :, :lane]
         pl.semaphore_wait(barrier, n_dev + n_grp - 2)
-        for d, (there, target) in enumerate(dirs):
-            @pl.when(there)
-            def _(d=d, target=target):
-                halo_copy(d, target).start()
+        start(0)
+        for j in range(0, 4 * halo, 2):
+            first = p_buf[near[8 + j % halo, j // halo], :, lane:]
+            second = p_buf[near[8 + j % halo + 1, j // halo], :, lane:]
+            tail_pack[j // 2] = jnp.concatenate([first, second], axis=1)
+        start(1)
+        pool[0:e_dev] = p_buf[:, :, :lane]
+        tail[0:e_dev] = p_buf[:, :, lane:]
 
     def halo_wait():
         for d, (there, target) in enumerate(dirs):
             @pl.when(there)
             def _(d=d, target=target):
-                halo_copy(d, target).wait_send()
-                pltpu.make_async_remote_copy(
-                    src_ref=pack.at[pl.ds(d * halo, halo)],
-                    dst_ref=pool.at[pl.ds(e_dev + d * halo, halo)],
-                    send_sem=h_send.at[d],
-                    recv_sem=h_recv.at[d],
-                    device_id=target,
-                    device_id_type=MESH,
-                ).wait_recv()
+                for part in range(2):
+                    halo_copy(part, d, target, d ^ 1).wait_send()
+                    halo_copy(part, d, target, d).wait_recv()
+                for j in range(d * halo // 2, (d + 1) * halo // 2):
+                    both = tail_in[j]
+                    tail[e_dev + 2 * j] = both[:, :rest_b]
+                    tail[e_dev + 2 * j + 1] = both[:, rest_b:]
 
     def left_of(k):
-        copies = a_copies(k)
-        for q, copy in enumerate(copies):
-            copy.wait()
-            size = e_dev // len(copies)
-
-            @pl.loop(q * size, (q + 1) * size, unroll=size)
-            def _(e):
-                rows = pl.ds(pl.multiple_of(e * width_c, width_c), width_c)
-                left[k, rows, :] = jnp.dot(
-                    turned[e], a_buf[k, e], preferred_element_type=F32
-                ).astype(BF16)
+        @pl.loop(0, e_dev, unroll=e_dev)
+        def _(e):
+            rows = pl.ds(pl.multiple_of(e * width_c, width_c), width_c)
+            left[k, rows, :] = jnp.dot(
+                turned[e], a_buf[k, e], preferred_element_type=F32
+            ).astype(BF16)
+
+    def a_wait(*ks):
+        for k in ks:
+            for copy in a_copies(k):
+                copy.wait()
 
     group_of_lane = iota((width_c, lane), 1) // width_c
     sub_lane = iota((sub, lane), 1) // width_c
@@ -291,7 +305,8 @@
         @pl.loop(0, groups, unroll=groups)
         def _(g):
             if k:
-                blocks = [pool[near[k - 1, g * rep + i]] for i in range(rep)]
+                at = [near[k - 1, g * rep + i] for i in range(rep)]
+                blocks = [jnp.concatenate([pool[i], tail[i]], axis=1) for i in at]
             else:
                 blocks = [p_buf[g * rep + i] for i in range(rep)]
             rows = pl.ds(pl.multiple_of(g * lane, lane), lane)
@@ -302,14 +317,14 @@
             picked = full[0:width_c]
             for i in range(1, rep):
                 picked = jnp.where(group_of_lane == i, full[i * width_c:(i + 1) * width_c], picked)
-            prod[k % 2, g] = picked
+            prod[k, g] = picked
 
     def right_sum(k):
         def masked(t):
             total = None
             for g in range(groups):
                 at = k * groups + g
-                term = jnp.where(code[at:at + 1, :] == t, prod[k % 2, g], 0.0)
+                term = jnp.where(code[at:at + 1, :] == t, prod[k, g], 0.0)
                 total = term if total is None else total + term
             return total
 
@@ -323,7 +338,81 @@
         p = place_of(k, n_k)
         for o in range(n_dev):
             parts[p, o] = part_t[own[1, o]]
-        inbox[p, dev] = parts[p, dev]
+        if p < early:
+            z_in[grp, p] = parts[p]
+        else:
+            inbox[p, dev] = parts[p, dev]
+
+    def column_copy(p, off):
+        return pltpu.make_async_remote_copy(
+            src_ref=parts.at[p],
+            dst_ref=z_in.at[grp, p],
+            send_sem=z_sem.at[0],
+            recv_sem=z_sem.at[1],
+            device_id=(lax.rem(grp + off, n_grp), dev),
+            device_id_type=MESH,
+        )
+
+    def column_all():
+        others = z_in.at[pl.ds(0, n_grp - 1)]
+        return pltpu.make_async_remote_copy(
+            src_ref=others,
+            dst_ref=others,
+            send_sem=z_sem.at[0],
+            recv_sem=z_sem.at[1],
+            device_id=(lax.rem(grp + 1, n_grp), dev),
+            device_id_type=MESH,
+        )
+
+    def column_start(p):
+        for off in range(1, n_grp):
+            column_copy(p, off).start()
+
+    def plane_copy(off):
+        target = lax.rem(dev + off, n_dev)
+        return pltpu.make_async_remote_copy(
+            src_ref=z_in.at[:, :, target],
+            dst_ref=y_in.at[dev],
+            send_sem=y_sem.at[0],
+            recv_sem=y_sem.at[1],
+            device_id=(grp, target),
+            device_id_type=MESH,
+        )
+
+    def plane_all():
+        others = y_in.at[pl.ds(0, n_dev - 1)]
+        return pltpu.make_async_remote_copy(
+            src_ref=others,
+            dst_ref=others,
+            send_sem=y_sem.at[0],
+            recv_sem=y_sem.at[1],
+            device_id=(grp, lax.rem(dev + 1, n_dev)),
+            device_id_type=MESH,
+        )
+
+    def plane_start():
+        column_all().wait_recv()
+        y_in[dev] = z_in[:, :, dev]
+        for off in range(1, n_dev):
+            plane_copy(off).start()
+
+    def early_place():
+        plane_all().wait_recv()
+
+        @pl.loop(0, n_grp, unroll=n_grp)
+        def _(g):
+            spots = [spot_of[pl.ds(g * n_dev + d, 1), :] for d in range(n_dev)]
+            for p in range(early):
+                values = [y_in[d, g, p].astype(F32) for d in range(n_dev)]
+                for j in range(group_rows):
+                    total = None
+                    for d in range(n_dev):
+                        term = jnp.where(spots[d] == j, values[d], 0.0)
+                        total = term if total is None else total + term
+                    early_rows[g * group_rows + j, p] = total.astype(BF16)
+
+        for p in range(early):
+            put_rows(early_rows, p, p + 1)
 
     def part_copy(c, off):
         start, size = chunks[c]
@@ -348,26 +437,80 @@
             device_id_type=MESH,
         )
 
-    def row_copy(c, off):
-        target = lax.rem(grp + off, n_grp)
-        return pltpu.make_async_remote_copy(
-            src_ref=gathered[c].at[pl.ds(grp * group_rows, group_rows)],
-            dst_ref=gathered[c].at[pl.ds(grp * group_rows, group_rows)],
+    def relayed(c):
+        return n_grp == 4 and c < 1
+
+    def block_of(c, sender):
+        return gathered[c].at[pl.ds(sender * group_rows, group_rows)]
+
+    def row_copy(c, sender, target, sem):
+        return pltpu.make_async_remote_copy(
+            src_ref=block_of(c, sender),
+            dst_ref=block_of(c, sender),
             send_sem=g_send.at[c],
-            recv_sem=g_recv.at[c],
+            recv_sem=sem,
             device_id=(target, dev),
             device_id_type=MESH,
         )
 
-    def row_all(c):
-        return pltpu.make_async_remote_copy(
-            src_ref=gathered[c].at[pl.ds(0, (n_grp - 1) * group_rows)],
-            dst_ref=gathered[c].at[pl.ds(0, (n_grp - 1) * group_rows)],
+    def row_all(c, count):
+        rows = gathered[c].at[pl.ds(0, count * group_rows)]
+        return pltpu.make_async_remote_copy(
+            src_ref=rows,
+            dst_ref=rows,
             send_sem=g_send.at[c],
             recv_sem=g_recv.at[c],
             device_id=(lax.rem(grp + 1, n_grp), dev),
             device_id_type=MESH,
         )
+
+    def send_rows(c):
+        if not relayed(c):
+            for off in range(1, n_grp):
+                row_copy(c, grp, lax.rem(grp + off, n_grp), g_recv.at[c]).start()
+            return
+        for g in range(4):
+            @pl.when(grp == g)
+            def _(g=g):
+                for target in sorted(range(4), key=lambda t: abs(t - g)):
+                    if 0 < abs(target - g) < 3:
+                        far = (g, target) in ((0, 2), (3, 1))
+                        row_copy(c, g, target, f_recv.at[c] if far else g_recv.at[c]).start()
+
+    def relay(c):
+        for g, sender in ((1, 3), (2, 0)):
+            @pl.when(grp == g)
+            def _(g=g, sender=sender):
+                row_copy(c, sender, g, f_recv.at[c]).wait_recv()
+                row_copy(c, sender, 3 - sender, g_recv.at[c]).start()
+
+    def rows_arrived(c):
+        if not relayed(c):
+            row_all(c, n_grp - 1).wait_recv()
+            return
+        inner = (grp == 1) | (grp == 2)
+
+        @pl.when(inner)
+        def _():
+            row_all(c, 2).wait_recv()
+
+        @pl.when(jnp.logical_not(inner))
+        def _():
+            row_all(c, 3).wait_recv()
+
+    def rows_sent(c):
+        if not relayed(c):
+            row_all(c, n_grp - 1).wait_send()
+            return
+        inner = (grp == 1) | (grp == 2)
+
+        @pl.when(inner)
+        def _():
+            row_all(c, 4).wait_send()
+
+        @pl.when(jnp.logical_not(inner))
+        def _():
+            row_all(c, 2).wait_send()
 
     def exchange(c):
         for off in range(1, n_dev):
@@ -383,8 +526,7 @@
                     member = jnp.where(own[2, d] == j, 1.0, 0.0).astype(F32)
                     total = total + inbox[start + i, d].astype(F32) * member
                 gathered[c][grp * group_rows + j, i] = total.astype(BF16)
-        for off in range(1, n_grp):
-            row_copy(c, off).start()
+        send_rows(c)
 
     def put_rows(rows, i, k):
         @pl.loop(0, rows_own, unroll=8)
@@ -397,15 +539,17 @@
             out_ref[k, :, j * lane:(j + 1) * lane] = flat[pl.ds(j, rows_own, stride=sub), :].astype(BF16)
 
     def place(c):
-        row_all(c).wait_recv()
+        rows_arrived(c)
         start, size = chunks[c]
         for i in range(size):
             put_rows(gathered[c], i, (start + i + 1) % n_k)
 
     def sent():
+        column_all().wait_send()
+        plane_all().wait_send()
         for c in range(len(chunks)):
             part_all(c).wait_send()
-            row_all(c).wait_send()
+            rows_sent(c)
 
     tables_one()
     a_first()
@@ -413,50 +557,49 @@
     p_wait()
     halo_start()
     turn_p()
+    a_wait(1)
     left_of(1)
+    a_wait(2)
     left_of(2)
     own_copy.wait()
+    a_wait(3)
     left_of(3)
+    a_wait(4)
     left_of(4)
     halo_wait()
     right_mm(1)
+    right_mm(2)
+    right_mm(3)
+    right_mm(4)
     right_sum(1)
+    right_sum(2)
+    right_sum(3)
+    right_sum(4)
+    column_start(0)
+    column_start(1)
     exchange(0)
-    right_mm(2)
-    right_sum(2)
+    a_wait(5,6)
+    left_of(5)
+    left_of(6)
+    right_mm(5)
+    right_mm(6)
+    right_sum(5)
+    right_sum(6)
     exchange(1)
-    left_of(5)
-    right_mm(3)
-    right_sum(3)
-    exchange(2)
-    left_of(6)
-    right_mm(4)
-    right_sum(4)
-    exchange(3)
-    right_mm(5)
-    right_sum(5)
-    exchange(4)
-    collect(0)
-    right_mm(6)
-    right_sum(6)
-    exchange(5)
-    collect(1)
+    a_wait(0)
     left_of(0)
     right_mm(0)
     right_sum(0)
-    exchange(6)
+    exchange(2)
+    collect(0)
+    collect(1)
     collect(2)
-    collect(3)
-    collect(4)
-    collect(5)
-    collect(6)
+    plane_start()
+    relay(0)
+    early_place()
     place(0)
     place(1)
     place(2)
-    place(3)
-    place(4)
-    place(5)
-    place(6)
     sent()
 
 
@@ -476,7 +619,8 @@
     groups = e_dev // rep
     chunks = chunks_of(n_k)
     n_chunks = len(chunks)
-    parted = 2
+    early = early_of(n_k)
+    parted = 1
     hbm = pl.BlockSpec(memory_space=pltpu.HBM)
     vmem = pl.BlockSpec(memory_space=pltpu.VMEM)
     ints = [nbr.T, nbr_agg.T, touch_agg.T, elem_slot.reshape(1, e_dev), coarse_row.reshape(1, -1)]
@@ -498,26 +642,36 @@
             pltpu.VMEM((n_k * groups, lane), jnp.int32),
             pltpu.VMEM((n_k, e_dev, width_b, width_b), BF16),
             pltpu.VMEM((e_dev, width_c, width_b), BF16),
-            pltpu.VMEM((e_dev + 4 * halo, width_c, width_b), BF16),
-            pltpu.VMEM((4 * halo, width_c, width_b), BF16),
+            pltpu.VMEM((e_dev + 4 * halo, width_c, lane), BF16),
+            pltpu.VMEM((e_dev + 4 * halo, width_c, width_b - lane), BF16),
+            pltpu.VMEM((4 * halo, width_c, lane), BF16),
+            pltpu.VMEM((2 * halo, width_c, lane), BF16),
+            pltpu.VMEM((2 * halo, width_c, lane), BF16),
             pltpu.VMEM((e_dev, width_c, width_b), BF16),
             pltpu.VMEM((n_k, e_dev * width_c, width_b), BF16),
-            pltpu.VMEM((2, groups, width_c, lane), F32),
+            pltpu.VMEM((n_k, groups, width_c, lane), F32),
             pltpu.VMEM((touch, width_c, lane), F32),
             pltpu.VMEM((touch + 1, sub, lane), BF16),
             pltpu.VMEM((n_k, n_dev, sub, lane), BF16),
             pltpu.VMEM((n_k, n_dev, sub, lane), BF16),
             pltpu.VMEM((rows_own * sub, lane), F32),
+            pltpu.VMEM((n_grp * n_dev, lane), jnp.int32),
+            pltpu.VMEM((n_grp, early, n_dev, sub, lane), BF16),
+            pltpu.VMEM((n_dev, n_grp, early, sub, lane), BF16),
+            pltpu.VMEM((rows_own, early, sub, lane), BF16),
         ] + [pltpu.VMEM((rows_own, size, sub, lane), BF16) for _, size in chunks] + [
             pltpu.SemaphoreType.DMA((n_k + parted - 1,)),
             pltpu.SemaphoreType.DMA((1,)),
             pltpu.SemaphoreType.DMA((2,)),
-            pltpu.SemaphoreType.DMA((4,)),
-            pltpu.SemaphoreType.DMA((4,)),
+            pltpu.SemaphoreType.DMA((8,)),
+            pltpu.SemaphoreType.DMA((8,)),
             pltpu.SemaphoreType.DMA((n_chunks,)),
             pltpu.SemaphoreType.DMA((n_chunks,)),
             pltpu.SemaphoreType.DMA((n_chunks,)),
             pltpu.SemaphoreType.DMA((n_chunks,)),
+            pltpu.SemaphoreType.DMA((n_chunks,)),
+            pltpu.SemaphoreType.DMA((2,)),
+            pltpu.SemaphoreType.DMA((2,)),
         ],
         compiler_params=pltpu.CompilerParams(
             collective_id=0, has_side_effects=True, vmem_limit_bytes=54656 * 1024

time: 25.8 us -> 24 us (0.930)
  Pallas kernels: 24 us -> 22.2 us
    pallas_call x1, Pallas kernels: 24 us -> 22.2 us  [on_device(): pl.pallas_call(functools.partial(kernel, n_grp, n_dev, halo, group_rows,...]
where the time goes in v4:
time: 24 us; the launch traced here: 23.8 us
  Pallas kernels  22.2 us (92%)
  other arithmetic  1.67 us (7%)
    pallas_call x1, Pallas kernels, on_device(): pl.pallas_call(functools.partial(kernel, n_grp, n_dev, halo, group_rows,...  22.2 us
    transpose x1, other arithmetic, on_device(): return out.astype(F32).transpose(1, 0, 2)  0.92 us
    add x1, other arithmetic, on_device(): sum((jnp.pad(x, ((8 * i, 8 * (len(ints) - i) - x.shape[0]), (0, width - x...  0.76 us

profile of v4, /device:TPU:0, one launch (start us, length us, event | category | flops | bytes accessed | tf_op | source)
XLA Modules:
  0.0 23.8 jit_solution(13584756785819918538)
XLA Ops:
  0.0 0.8 %pad_add_fusion.packed = s32[40,256]{1,0:T(8,128)S(1)} fusion(s32[1,136]{1,0:T(1,128)} %bitcast.10, s32[1,32]{1,0:T(1,128)} %bitcast.11, s32[6,32]{1,0:T(8,128)} %bitcast.7, s32[6,32]{1,0:T(8,128)} %bitcast.8, s32[6,32]{1,0:T(8,128)} %bitcast.9), kind=kLoop, calls=%fused_computation.1 | loop fusion | flops 40960 | bytes 43936 | tf_op jit(solution)/shard_map/add | solution.py:628
  0.8 22.2 %galerkin.1 = bf16[7,24,1024]{2,1,0:T(8,128)(2,1)S(1)} custom-call(bf16[32,7,192,192]{3,2,1,0:T(8,128)(2,1)} %a_ref.1, bf16[32,32,192]{2,1,0:T(8,128)(2,1)} %p_ref.1, s32[40,256]{1,0:T(8,128)S(1)} %pad_add_fusion.packed), custom_call_target="tpu_custom_call" | custom-call | tf_op jit(solution)/shard_map/galerkin/pallas_call | solution.py:632
  22.9 0.9 %convert_bitcast_fusion = f32[24,7,1024]{2,0,1:T(8,128)} fusion(bf16[7,24,1024]{2,1,0:T(8,128)(2,1)S(1)} %galerkin.1), kind=kLoop, calls=%fused_computation | loop fusion | flops 172032 | bytes 1032192 | tf_op jit(solution)/shard_map/transpose | solution.py:681

commit v5 on v4

--- a/solution.py
+++ b/solution.py
@@ -161,11 +161,11 @@
     parted = a_sem.shape[0] - n_k + 1
 
     def a_copies(k):
-        count = parted if k == 1 else 1
+        count = parted if k == 0 else 1
         size = e_dev // count
         return [
             pltpu.make_async_copy(
-                a_ref.at[pl.ds(q * size, size), k], a_buf.at[k, pl.ds(q * size, size)], a_sem.at[place_of(k, n_k) + (q if k == 1 else parted - 1)]
+                a_ref.at[pl.ds(q * size, size), k], a_buf.at[k, pl.ds(q * size, size)], a_sem.at[place_of(k, n_k) + q]
             )
             for q in range(count)
         ]
@@ -273,8 +273,10 @@
                     tail[e_dev + 2 * j] = both[:, :rest_b]
                     tail[e_dev + 2 * j + 1] = both[:, rest_b:]
 
-    def left_of(k):
-        @pl.loop(0, e_dev, unroll=e_dev)
+    def left_of(k, part=0, count=1):
+        size = e_dev // count
+
+        @pl.loop(part * size, (part + 1) * size, unroll=size)
         def _(e):
             rows = pl.ds(pl.multiple_of(e * width_c, width_c), width_c)
             left[k, rows, :] = jnp.dot(
@@ -301,8 +303,10 @@
             out = picked if out is None else out + picked
         return out
 
-    def right_mm(k):
-        @pl.loop(0, groups, unroll=groups)
+    def right_mm(k, part=0, count=1):
+        size = groups // count
+
+        @pl.loop(part * size, (part + 1) * size, unroll=size)
         def _(g):
             if k:
                 at = [near[k - 1, g * rep + i] for i in range(rep)]
@@ -318,6 +322,12 @@
             for i in range(1, rep):
                 picked = jnp.where(group_of_lane == i, full[i * width_c:(i + 1) * width_c], picked)
             prod[k, g] = picked
+
+    def own_last():
+        for q, copy in enumerate(a_copies(0)):
+            copy.wait()
+            left_of(0, q, parted)
+            right_mm(0, q, parted)
 
     def right_sum(k):
         def masked(t):
@@ -575,9 +585,9 @@
     right_sum(2)
     right_sum(3)
     right_sum(4)
+    exchange(0)
     column_start(0)
     column_start(1)
-    exchange(0)
     a_wait(5,6)
     left_of(5)
     left_of(6)
@@ -592,14 +602,14 @@
     right_sum(0)
     exchange(2)
     collect(0)
+    plane_start()
     collect(1)
     collect(2)
-    plane_start()
     relay(0)
     early_place()
-    place(0)
     place(1)
     place(2)
+    place(0)
     sent()
 
 

time: 24 us -> 24.2 us (level)
  no operation moved by 1% of the time
where the time goes in v5:
time: 24.2 us; the launch traced here: 24 us
  Pallas kernels  22.3 us (92%)
  other arithmetic  1.67 us (7%)
    pallas_call x1, Pallas kernels, on_device(): pl.pallas_call(functools.partial(kernel, n_grp, n_dev, halo, group_rows,...  22.3 us
    transpose x1, other arithmetic, on_device(): return out.astype(F32).transpose(1, 0, 2)  0.92 us
    add x1, other arithmetic, on_device(): sum((jnp.pad(x, ((8 * i, 8 * (len(ints) - i) - x.shape[0]), (0, width - x...  0.76 us

profile of v5, /device:TPU:0, one launch (start us, length us, event | category | flops | bytes accessed | tf_op | source)
XLA Modules:
  0.0 24.0 jit_solution(2037280867763986258)
XLA Ops:
  0.0 0.8 %pad_add_fusion.packed = s32[40,256]{1,0:T(8,128)S(1)} fusion(s32[1,136]{1,0:T(1,128)} %bitcast.10, s32[1,32]{1,0:T(1,128)} %bitcast.11, s32[6,32]{1,0:T(8,128)} %bitcast.7, s32[6,32]{1,0:T(8,128)} %bitcast.8, s32[6,32]{1,0:T(8,128)} %bitcast.9), kind=kLoop, calls=%fused_computation.1 | loop fusion | flops 40960 | bytes 43936 | tf_op jit(solution)/shard_map/add | solution.py:638
  0.8 22.3 %galerkin.1 = bf16[7,24,1024]{2,1,0:T(8,128)(2,1)S(1)} custom-call(bf16[32,7,192,192]{3,2,1,0:T(8,128)(2,1)} %a_ref.1, bf16[32,32,192]{2,1,0:T(8,128)(2,1)} %p_ref.1, s32[40,256]{1,0:T(8,128)S(1)} %pad_add_fusion.packed), custom_call_target="tpu_custom_call" | custom-call | tf_op jit(solution)/shard_map/galerkin/pallas_call | solution.py:642
  23.1 0.9 %convert_bitcast_fusion = f32[24,7,1024]{2,0,1:T(8,128)} fusion(bf16[7,24,1024]{2,1,0:T(8,128)(2,1)S(1)} %galerkin.1), kind=kLoop, calls=%fused_computation | loop fusion | flops 172032 | bytes 1032192 | tf_op jit(solution)/shard_map/transpose | solution.py:691

commit v6 on v5

--- a/solution.py
+++ b/solution.py
@@ -131,11 +131,16 @@
     spot_of[...] = jnp.broadcast_to(spots, spot_of.shape)
     peer = iota((devices, n_dev), 1) + grp * n_dev
     put(2, where_sum(peer == iota((devices, n_dev), 0), spots, 0))
-    inverse = jnp.full((1, n_dev), touch, jnp.int32)
-    for t in range(touch):
-        own = where_sum(row == device, owners[t], 0)
-        inverse = jnp.where(own == iota((1, n_dev), 1), t, inverse)
-    put(1, inverse)
+    def inverse_of(which):
+        inverse = jnp.full((1, n_dev), touch, jnp.int32)
+        for t in range(touch):
+            own = where_sum(row == which, owners[t], 0)
+            inverse = jnp.where(own == iota((1, n_dev), 1), t, inverse)
+        return inverse
+
+    put(1, inverse_of(device))
+    for g in range(devices // n_dev):
+        put(8 + g, inverse_of(g * n_dev + dev))
 
 
 def kernel(
@@ -143,7 +148,7 @@
     a_ref, p_ref, packed,
     out_ref,
     near_v, own_v, near, own, code,
-    a_buf, p_buf, pool, tail, pack, tail_pack, tail_in, turned, left, prod, same_sum, part_t, parts, inbox, flat, spot_of, z_in, y_in, early_rows,
+    a_buf, p_buf, pool, tail, pack, tail_pack, tail_in, turned, left, prod, same_sum, part_t, parts, inbox, flat, spot_of, z_in, z_out, y_out, y_in, early_rows,
     *rest,
 ):
     *gathered, a_sem, p_sem, t_sem, h_send, h_recv, x_send, x_recv, g_send, g_recv, f_recv, z_sem, y_sem = rest
@@ -219,6 +224,9 @@
             nbr, nbr_agg, slot, touch_agg, coarse_row, own_v, code, spot_of,
         )
         part_t[touch] = jnp.zeros(part_t.shape[1:], BF16)
+        for g in range(n_grp):
+            for p in range(early):
+                z_in[g, p, touch] = jnp.zeros(part_t.shape[1:], BF16)
         own_copy.start()
 
     def a_first():
@@ -338,25 +346,28 @@
                 total = term if total is None else total + term
             return total
 
+        p = place_of(k, n_k)
         for t in range(touch):
             together = masked(t + touch)
             if k != 1:
                 together = same_sum[t] + together
             if k:
                 same_sum[t] = together
-            part_t[t] = squeeze(masked(t) if k else together).astype(BF16)
-        p = place_of(k, n_k)
-        for o in range(n_dev):
-            parts[p, o] = part_t[own[1, o]]
-        if p < early:
-            z_in[grp, p] = parts[p]
-        else:
+            value = squeeze(masked(t) if k else together).astype(BF16)
+            if p < early:
+                z_out[p, t] = value
+                z_in[grp, p, t] = value
+            else:
+                part_t[t] = value
+        if p >= early:
+            for o in range(n_dev):
+                parts[p, o] = part_t[own[1, o]]
             inbox[p, dev] = parts[p, dev]
 
     def column_copy(p, off):
         return pltpu.make_async_remote_copy(
-            src_ref=parts.at[p],
-            dst_ref=z_in.at[grp, p],
+            src_ref=z_out.at[p],
+            dst_ref=z_in.at[grp, p, pl.ds(0, touch)],
             send_sem=z_sem.at[0],
             recv_sem=z_sem.at[1],
             device_id=(lax.rem(grp + off, n_grp), dev),
@@ -364,7 +375,7 @@
         )
 
     def column_all():
-        others = z_in.at[pl.ds(0, n_grp - 1)]
+        others = z_in.at[pl.ds(0, n_grp - 1), :, pl.ds(0, touch)]
         return pltpu.make_async_remote_copy(
             src_ref=others,
             dst_ref=others,
@@ -381,7 +392,7 @@
     def plane_copy(off):
         target = lax.rem(dev + off, n_dev)
         return pltpu.make_async_remote_copy(
-            src_ref=z_in.at[:, :, target],
+            src_ref=y_out.at[target],
             dst_ref=y_in.at[dev],
             send_sem=y_sem.at[0],
             recv_sem=y_sem.at[1],
@@ -402,7 +413,11 @@
 
     def plane_start():
         column_all().wait_recv()
-        y_in[dev] = z_in[:, :, dev]
+        for o in range(n_dev):
+            for g in range(n_grp):
+                for p in range(early):
+                    y_out[o, g, p] = z_in[g, p, own[8 + g, o]]
+        y_in[dev] = y_out[dev]
         for off in range(1, n_dev):
             plane_copy(off).start()
 
@@ -607,9 +622,9 @@
     collect(2)
     relay(0)
     early_place()
+    place(0)
     place(1)
     place(2)
-    place(0)
     sent()
 
 
@@ -646,9 +661,9 @@
         out_specs=vmem,
         scratch_shapes=[
             pltpu.VMEM((16, lane), jnp.int32),
-            pltpu.VMEM((8, lane), jnp.int32),
+            pltpu.VMEM((8 + -(-n_grp // 8) * 8, lane), jnp.int32),
             pltpu.SMEM((16, lane), jnp.int32),
-            pltpu.SMEM((8, lane), jnp.int32),
+            pltpu.SMEM((8 + -(-n_grp // 8) * 8, lane), jnp.int32),
             pltpu.VMEM((n_k * groups, lane), jnp.int32),
             pltpu.VMEM((n_k, e_dev, width_b, width_b), BF16),
             pltpu.VMEM((e_dev, width_c, width_b), BF16),
@@ -666,7 +681,9 @@
             pltpu.VMEM((n_k, n_dev, sub, lane), BF16),
             pltpu.VMEM((rows_own * sub, lane), F32),
             pltpu.VMEM((n_grp * n_dev, lane), jnp.int32),
-            pltpu.VMEM((n_grp, early, n_dev, sub, lane), BF16),
+            pltpu.VMEM((n_grp, early, touch + 1, sub, lane), BF16),
+            pltpu.VMEM((early, touch, sub, lane), BF16),
+            pltpu.VMEM((n_dev, n_grp, early, sub, lane), BF16),
             pltpu.VMEM((n_dev, n_grp, early, sub, lane), BF16),
             pltpu.VMEM((rows_own, early, sub, lane), BF16),
         ] + [pltpu.VMEM((rows_own, size, sub, lane), BF16) for _, size in chunks] + [

time: 24.2 us -> 24.1 us (level)
  no operation moved by 1% of the time
where the time goes in v6:
time: 24.1 us; the launch traced here: 23.9 us
  Pallas kernels  22.2 us (92%)
  other arithmetic  1.67 us (7%)
    pallas_call x1, Pallas kernels, on_device(): pl.pallas_call(functools.partial(kernel, n_grp, n_dev, halo, group_rows,...  22.2 us
    transpose x1, other arithmetic, on_device(): return out.astype(F32).transpose(1, 0, 2)  0.92 us
    add x1, other arithmetic, on_device(): sum((jnp.pad(x, ((8 * i, 8 * (len(ints) - i) - x.shape[0]), (0, width - x...  0.76 us

profile of v6, /device:TPU:0, one launch (start us, length us, event | category | flops | bytes accessed | tf_op | source)
XLA Modules:
  0.0 23.9 jit_solution(3996327678291259151)
XLA Ops:
  0.0 0.8 %pad_add_fusion.packed = s32[40,256]{1,0:T(8,128)S(1)} fusion(s32[1,136]{1,0:T(1,128)} %bitcast.10, s32[1,32]{1,0:T(1,128)} %bitcast.11, s32[6,32]{1,0:T(8,128)} %bitcast.7, s32[6,32]{1,0:T(8,128)} %bitcast.8, s32[6,32]{1,0:T(8,128)} %bitcast.9), kind=kLoop, calls=%fused_computation.1 | loop fusion | flops 40960 | bytes 43936 | tf_op jit(solution)/shard_map/add | solution.py:653
  0.8 22.2 %galerkin.1 = bf16[7,24,1024]{2,1,0:T(8,128)(2,1)S(1)} custom-call(bf16[32,7,192,192]{3,2,1,0:T(8,128)(2,1)} %a_ref.1, bf16[32,32,192]{2,1,0:T(8,128)(2,1)} %p_ref.1, s32[40,256]{1,0:T(8,128)S(1)} %pad_add_fusion.packed), custom_call_target="tpu_custom_call" | custom-call | tf_op jit(solution)/shard_map/galerkin/pallas_call | solution.py:657
  23.0 0.9 %convert_bitcast_fusion = f32[24,7,1024]{2,0,1:T(8,128)} fusion(bf16[7,24,1024]{2,1,0:T(8,128)(2,1)S(1)} %galerkin.1), kind=kLoop, calls=%fused_computation | loop fusion | flops 172032 | bytes 1032192 | tf_op jit(solution)/shard_map/transpose | solution.py:708
